TPU v7x, 128 devices: a whole 4x4x4 slice. The times are simulated.
128 devices in a mesh: seq: 16 (over y, x), kvh: 8 (over z, core).
Axes of the slice: x: 4, y: 4, z: 4, core: 2. Of those that a mesh axis runs over, the one named last changes fastest.
Arguments:
- queries: bfloat16 [64, 64, 128], P(None, 'kvh'), may hold values from -128 to 128
- keys: bfloat16 [2048, 8, 128, 128], P('seq', 'kvh'), may hold values from -6 to 6
- values: bfloat16 [2048, 8, 128, 128], P('seq', 'kvh'), may hold values from -6 to 6
- rep_keys: bfloat16 [2048, 8, 4, 128], P('seq', 'kvh'), may hold values from -8 to 8
- rep_values: bfloat16 [2048, 8, 4, 128], P('seq', 'kvh'), may hold values from -6 to 6
- block_ids: int32 [64, 8, 16], P(None, 'kvh'), may hold values from 0 to 2047, as said below
- block_counts: int32 [2048], P('seq'), may hold values from 64 to 128
- out_weight: bfloat16 [8192, 8192], P('kvh', 'seq'), may hold values from -0.5 to 0.5
Outputs:
- projected: bfloat16 [64, 8192], P('kvh', 'seq')
Inputs may be any that keep to these rules, and one draw needn't show every extreme that they name: `block_ids`: for every token and key-value head the 16 ids are different. For every key-value head at most 192 of its 64 x 16 ids lie among the blocks o * 128 to (o + 1) * 128 - 1 of one o, and for some o exactly 192.
All inputs are finite; a program needn't handle non-finite values.
Results may differ from a plain program's by a relative error of at most 0.023.
Values may be sent and summed in bfloat16 or wider, within the bound.
A program may use at most 128 MiB of HBM per device.

v0:
```python
import math

import jax
import jax.numpy as jnp
from jax import lax
from jax.sharding import Mesh
from jax.sharding import PartitionSpec as P

SEQ = ("seq_0", "seq_1")


FLOOR_SCORE = -1e30


def collected_together(value, axis):
    leaves = jax.tree.leaves(value)
    turns = sorted(range(len(leaves)), key=lambda k: -leaves[k].size)
    width = (1, *leaves[turns[0]].shape)[-1]
    lines = [
        jnp.pad(leaves[k].reshape(-1), (0, -leaves[k].size % width)).reshape(-1, width)
        for k in turns
    ]
    both, at, found = (lax.all_gather(jnp.concatenate(lines), axis), 0, {})
    for k, line in zip(turns, lines):
        share = both[:, at : at + len(line)].reshape(len(both), -1)
        found[k] = share[:, : leaves[k].size].reshape(-1, *leaves[k].shape)
        at += len(line)
    numbers = iter(range(len(leaves)))
    return jax.tree.map(lambda _: found[next(numbers)], value)


def combined_by_axis(value, axes, combine):
    for axis in axes:
        pieces = collected_together(
            jax.tree.map(
                lambda part, kind: part.astype(kind),
                value,
                jax.tree.map(lambda a: jnp.bfloat16 if a.dtype == jnp.float32 else a.dtype, value),
            ),
            axis,
        )
        widened = [
            jax.tree.map(lambda part, own: part[k].astype(own.dtype), pieces, value)
            for k in range(lax.axis_size(axis))
        ]
        value = widened[0]
        for received in widened[1:]:
            value = combine(value, received)
    return value


def in_blocks(value, dim, devices):
    shape = value.shape
    parts = value.reshape(*shape[:dim], devices, shape[dim] // devices, *shape[dim + 1 :])
    return jnp.moveaxis(parts, dim, 0)


def sum_at_owner(value, axis, dim):
    devices = lax.axis_size(axis)
    parts = lax.all_to_all(in_blocks(value, dim, devices), axis, 0, 0, tiled=True)
    return jnp.sum(parts.astype(jnp.float32), axis=0)


def combine(former, latter):
    highest = jnp.maximum(former[0], latter[0])
    first_factor = jnp.exp(former[0] - highest)
    second_factor = jnp.exp(latter[0] - highest)
    weight_sum = former[1] * first_factor + latter[1] * second_factor
    weighted = former[2] * first_factor[..., None] + latter[2] * second_factor[..., None]
    return (highest, weight_sum, weighted)


def summary_stats(query_rows, summary_keys, summary_vals):
    inv_root = 1.0 / math.sqrt(query_rows.shape[-1])
    scores = (
        jnp.einsum("bkgd,nkrd->bkgrn", query_rows, summary_keys, preferred_element_type=jnp.float32)
        * inv_root
    )
    highest = jnp.max(scores, axis=(3, 4))
    weights = jnp.exp(scores - highest[..., None, None])
    weight_sum = jnp.sum(weights, axis=(3, 4))
    weighted = jnp.einsum(
        "bkgrn,nkrd->bkgd",
        weights.astype(jnp.bfloat16),
        summary_vals,
        preferred_element_type=jnp.float32,
    )
    return (highest, weight_sum, weighted)


def chosen_stats(query_rows, tile_keys, tile_vals, slot_token, slot_count, slot_live):
    num_tokens = query_rows.shape[0]
    block_width = tile_keys.shape[2]
    inv_root = 1.0 / math.sqrt(query_rows.shape[-1])
    heads_here = jnp.arange(tile_keys.shape[0], dtype=jnp.int32)
    slot_query = query_rows[slot_token, heads_here[:, None]]
    scores = (
        jnp.einsum("kjgd,kjtd->kjgt", slot_query, tile_keys, preferred_element_type=jnp.float32)
        * inv_root
    )
    inside = jnp.arange(block_width, dtype=jnp.int32)[None, None, :] < slot_count[:, :, None]
    allowed = (inside & slot_live[:, :, None])[:, :, None, :]
    scores = jnp.where(allowed, scores, FLOOR_SCORE)
    slot_max = jnp.max(scores, axis=3)
    owner_map = slot_token[None, :, :] == jnp.arange(num_tokens, dtype=jnp.int32)[:, None, None]
    highest = jnp.max(jnp.where(owner_map[..., None], slot_max[None], FLOOR_SCORE), axis=2)
    slot_high = highest[slot_token, heads_here[:, None]]
    weights = jnp.where(allowed, jnp.exp(scores - slot_high[..., None]), 0.0)
    token_onehot = owner_map.astype(jnp.float32)
    weight_sum = jnp.einsum(
        "bkj,kjg->bkg", token_onehot, jnp.sum(weights, axis=3), precision=lax.Precision.HIGHEST
    )
    slot_weighted = jnp.einsum(
        "kjgt,kjtd->kjgd",
        weights.astype(jnp.bfloat16),
        tile_vals,
        preferred_element_type=jnp.float32,
    )
    weighted = jnp.einsum(
        "bkj,kjgd->bkgd", token_onehot, slot_weighted, precision=lax.Precision.HIGHEST
    )
    return (highest, weight_sum, weighted)


def on_device(queries, keys, values, rep_keys, rep_values, block_ids, block_counts, out_weight):
    num_tokens = queries.shape[0]
    local_heads = keys.shape[1]
    blocks_here = keys.shape[0]
    chosen_count = block_ids.shape[2]
    query_rows = queries.reshape(num_tokens, local_heads, -1, queries.shape[2])
    seq_index = lax.axis_index(SEQ)
    flat_ids = jnp.transpose(block_ids, (1, 0, 2)).reshape(local_heads, num_tokens * chosen_count)
    pair_token = jnp.arange(num_tokens * chosen_count, dtype=jnp.int32) // chosen_count
    head_pos = jnp.arange(local_heads, dtype=jnp.int32)
    capacity = 3 * num_tokens
    local_pair = flat_ids // blocks_here == seq_index
    local_rank = jnp.cumsum(local_pair.astype(jnp.int32), axis=1) - 1
    slot_ids = jnp.arange(capacity, dtype=jnp.int32)
    chosen_map = local_pair[:, None, :] & (local_rank[:, None, :] == slot_ids[None, :, None])
    slot_live = jnp.any(chosen_map, axis=2)
    slot_block = jnp.sum(jnp.where(chosen_map, flat_ids[:, None, :] % blocks_here, 0), axis=2)
    slot_token = jnp.sum(jnp.where(chosen_map, pair_token[None, None, :], 0), axis=2)
    tile_keys = keys[slot_block, head_pos[:, None]]
    tile_vals = values[slot_block, head_pos[:, None]]
    slot_count = block_counts[slot_block]
    chosen = chosen_stats(query_rows, tile_keys, tile_vals, slot_token, slot_count, slot_live)
    partial_value = combine(summary_stats(query_rows, rep_keys, rep_values), chosen)
    merged = combined_by_axis(partial_value, SEQ, combine)
    attended = (merged[2] / merged[1][..., None]).astype(jnp.bfloat16).reshape(num_tokens, -1)
    terms = jnp.dot(attended, out_weight, preferred_element_type=jnp.float32)
    return sum_at_owner(terms.astype(jnp.bfloat16), "kvh", 0).astype(jnp.bfloat16)


def solution(mesh):
    split = Mesh(mesh.devices.reshape(4, 4, mesh.shape["kvh"]), ("seq_0", "seq_1", "kvh"))
    in_specs = (
        P(None, "kvh", None),
        P(SEQ, "kvh", None, None),
        P(SEQ, "kvh", None, None),
        P(SEQ, "kvh", None, None),
        P(SEQ, "kvh", None, None),
        P(None, "kvh", None),
        P(SEQ),
        P("kvh", SEQ),
    )
    out_specs = P("kvh", SEQ)
    return jax.shard_map(
        on_device, mesh=split, in_specs=in_specs, out_specs=out_specs, check_vma=False
    )
```

profile of v0, /device:TPU:1, one launch (start us, length us, event | category | flops | bytes accessed | tf_op | source)
XLA Modules:
  0.0 83.6 jit_solution(16965377199651194661)
XLA Ops:
  0.0 0.0 copy-start
  0.0 0.9 %copy.49 = s32[64,1,16]{2,0,1:T(8,128)S(1)} copy(s32[64,1,16]{0,2,1:T(8,128)} %param.13) | data formatting | bytes 8192 | tf_op args[5]
  0.9 0.1 reshape_transpose.6
  0.9 0.1 reshape_transpose.5
  1.1 0.3 reduce-window.6
  1.4 0.2 slice_reduce_fusion
  1.5 0.2 reduce-window.9
  1.7 0.1 broadcast.585
  1.8 0.2 fusion.16
  2.0 0.4 select_reduce_fusion
  2.5 1.9 %gather_fusion = s32[192]{0:T(256)S(1)} fusion(s32[128]{0:T(128)} %param.14, s32[1024]{0:T(1024)S(1)} %pad_clamp_fusion), kind=kCustom, calls=%fused_computation | custom fusion | bytes 2304 | tf_op jit(solution)/shard_map/gather | solution.py:145
  4.4 0.1 fusion.42
  4.5 2.0 %gather_fusion.1 = bf16[192,8,128]{2,1,0:T(8,128)(2,1)S(1)} fusion(bf16[64,1,8,128]{3,2,0,1:T(8,128)(2,1)} %bitcast.404, s32[192]{0:T(256)S(1)} %bitcast.397), kind=kCustom, calls=%fused_computation.1 | custom fusion | bytes 787968 | tf_op jit(solution)/shard_map/gather | solution.py:96
  6.6 10.5 %gather_fusion.2 = bf16[192,128,128]{2,1,0:T(8,128)(2,1)} fusion(bf16[128,1,128,128]{3,2,1,0:T(8,128)(2,1)} %param.9, s32[192]{0:T(256)S(1)} %bitcast.395), kind=kCustom, calls=%fused_computation.2 | custom fusion | bytes 12584448 | tf_op jit(solution)/shard_map/gather | solution.py:143
  17.1 0.0 copy-start.1
  17.1 0.0 copy-start.2
  17.1 5.6 %fusion.109 = (f32[192,8]{1,0:T(8,128)S(1)}, f32[192,8,128]{2,1,0:T(8,128)S(1)}) fusion(bf16[192,8,128]{2,1,0:T(8,128)(2,1)S(1)} %gather_fusion.1, bf16[192,128,128]{2,1,0:T(8,128)(2,1)} %gather_fusion.2, pred[192,128]{1,0:T(8,128)(4,1)S(1)} %fusion.42), kind=kOutput, calls=%fused_computation.206 | convolution fusion | flops 50919936 | bytes 7501824 | tf_op jit(solution)/shard_map/kjgd,kjtd->kjgt/dot_general | solution.py:98
  22.6 0.1 copy.51
  22.7 0.2 select_reduce_fusion.2
  22.9 0.1 copy.52
  22.9 0.0 copy-done.1
  22.9 0.0 copy-done.2
  22.9 0.4 fusion.110
  23.4 0.1 copy.55
  23.4 1.1 %gather_fusion.3 = f32[192,8]{1,0:T(8,128)S(1)} fusion(f32[64,1,8]{2,1,0:T(1,128)S(1)} %copy.55, s32[192]{0:T(256)S(1)} %bitcast.398), kind=kCustom, calls=%fused_computation.3 | custom fusion | bytes 13824 | tf_op jit(solution)/shard_map/gather | solution.py:107
  24.5 10.3 %gather_fusion.4 = bf16[192,128,128]{2,1,0:T(8,128)(2,1)} fusion(bf16[128,1,128,128]{3,2,1,0:T(8,128)(2,1)} %param.10, s32[192]{0:T(256)S(1)} %bitcast.396), kind=kCustom, calls=%fused_computation.4 | custom fusion | bytes 12584448 | tf_op jit(solution)/shard_map/gather | solution.py:144
  34.8 0.0 copy-start.3
  34.8 0.5 fusion.17
  35.3 3.9 %fusion.21 = f32[192,8,128]{2,1,0:T(8,128)S(1)} fusion(bf16[192,128,128]{2,1,0:T(8,128)(2,1)} %gather_fusion.4, f32[192,8,128]{2,1,0:T(8,128)S(1)} %get-tuple-element.39, f32[192,8]{1,0:T(8,128)S(1)} %gather_fusion.3, pred[192,128]{1,0:T(8,128)(4,1)S(1)} %fusion.42), kind=kOutput, calls=%fused_computation.37 | convolution fusion | flops 50921472 | bytes 7895040 | tf_op jit(solution)/shard_map/kjgt,kjtd->kjgd/dot_general | solution.py:113
  39.2 0.5 fusion.13
  39.7 0.1 copy.53
  39.8 0.1 copy.59
  39.9 0.4 fusion.19
  40.2 0.2 fusion.10
  40.5 0.1 copy.61
  40.6 0.1 reshape.1324
  40.7 0.1 copy.60
  40.8 0.1 convert_element_type.485
  40.9 0.0 copy-done.3
  40.9 0.5 fusion.6
  41.4 12.6 %all-gather = bf16[2080,128]{1,0:T(8,128)(2,1)S(1)} all-gather(bf16[520,128]{1,0:T(8,128)(2,1)S(1)} %pad_maximum_fusion), channel_id=2, replica_groups=mesh['seq_0'=4,'seq_1'=4,'kvh'=8] {'seq_0'}, dimensions={0}, use_global_device_ids=true | all-gather | bytes 665600 | tf_op jit(solution)/shard_map/all_gather | solution.py:23
  54.1 0.5 fusion.31
  54.6 10.4 %all-gather.1 = bf16[2080,128]{1,0:T(8,128)(2,1)S(1)} all-gather(bf16[520,128]{1,0:T(8,128)(2,1)S(1)} %pad_maximum_fusion.1), channel_id=3, replica_groups=mesh['seq_0'=4,'seq_1'=4,'kvh'=8] {'seq_1'}, dimensions={0}, use_global_device_ids=true | all-gather | bytes 665600 | tf_op jit(solution)/shard_map/all_gather | solution.py:23
  64.9 0.1 slice_convert_fusion.3
  65.2 0.1 reshape.1343
  65.3 0.1 reshape.1344
  65.4 0.1 reshape.1346
  65.5 0.1 reshape.1348
  65.6 0.1 reshape.1350
  65.7 0.1 reshape.1351
  65.8 0.1 reshape.1352
  65.9 0.1 reshape.1353
  66.0 0.1 mul.321
  66.2 0.1 mul.324
  66.3 0.1 mul.327
  66.4 0.1 mul.330
  66.6 0.1 mul.333
  66.7 0.1 mul.336
  66.8 0.1 div.51
  67.0 0.0 copy-done
  67.0 0.5 fusion.7
  67.5 15.5 %all_to_all.5 = bf16[8,8,512]{2,1,0:T(8,128)(2,1)S(1)} all-to-all(bf16[8,8,512]{2,1,0:T(8,128)(2,1)S(1)} %fusion.7), channel_id=1, replica_groups=mesh['seq_0'=4,'seq_1'=4,'kvh'=8] {'kvh'}, dimensions={0} | all-to-all | bytes 131072 | tf_op jit(solution)/shard_map/all_to_all | solution.py:60
  83.0 0.6 reduce_sum.61
  (25 shorter events, 0.4 us)
Async XLA Ops:
  0.0 67.0 %copy-start = (bf16[1024,512]{1,0:T(8,128)(2,1)S(1)}, bf16[1024,512]{1,0:T(8,128)(2,1)}, u32[]{:S(2)}) copy-start(bf16[1024,512]{1,0:T(8,128)(2,1)} %param.15) | copy-start | bytes 3145732
  17.1 5.9 %copy-start.1 = (bf16[64,8,128]{2,1,0:T(8,128)(2,1)S(1)}, bf16[64,8,128]{2,1,0:T(8,128)(2,1)}, u32[]{:S(2)}) copy-start(bf16[64,8,128]{2,1,0:T(8,128)(2,1)} %param.8) | copy-start | bytes 393220
  17.1 5.9 %copy-start.2 = (bf16[128,1,4,128]{3,2,1,0:T(4,128)(2,1)S(1)}, bf16[128,1,4,128]{3,2,1,0:T(4,128)(2,1)}, u32[]{:S(2)}) copy-start(bf16[128,1,4,128]{3,2,1,0:T(4,128)(2,1)} %param.11) | copy-start | bytes 393220
  34.8 6.1 %copy-start.3 = (bf16[128,1,4,128]{3,2,1,0:T(4,128)(2,1)S(1)}, bf16[128,1,4,128]{3,2,1,0:T(4,128)(2,1)}, u32[]{:S(2)}) copy-start(bf16[128,1,4,128]{3,2,1,0:T(4,128)(2,1)} %param.12) | copy-start | bytes 393220
where the time goes:
time: 84 us; the launch traced here: 83.6 us
  blocking collectives  38.5 us (46%)
  local copies, waits for them, and re-layouts  29.6 us (35%)
  matrix products  11.5 us (14%)
  other arithmetic  3.6 us (4%)
    all_gather x2, blocking collectives, collected_together(): both, at, found = (lax.all_gather(jnp.concatenate(lines), axis), 0, {})  23 us
    all_to_all x1, blocking collectives, sum_at_owner(): lax.all_to_all(in_blocks(value, dim, devices), axis, 0, 0, tiled=True)  15.5 us
    gather x1, local copies, waits for them, and re-layouts, on_device(): tile_keys = keys[slot_block, head_pos[:, None]]  10.5 us
    gather x1, local copies, waits for them, and re-layouts, on_device(): tile_vals = values[slot_block, head_pos[:, None]]  10.3 us
    dot_general x1, matrix products, chosen_stats(): jnp.einsum('kjgd,kjtd->kjgt', slot_query, tile_keys, preferred_element_ty...  5.56 us
    dot_general x1, matrix products, chosen_stats(): jnp.einsum('kjgt,kjtd->kjgd', weights.astype(jnp.bfloat16), tile_vals, pr...  3.88 us
    gather x1, local copies, waits for them, and re-layouts, chosen_stats(): slot_query = query_rows[slot_token, heads_here[:, None]]  2.04 us
    gather x1, local copies, waits for them, and re-layouts, on_device(): slot_count = block_counts[slot_block]  1.89 us

commit v1 on v0

v1 whole, which is shorter than its diff:
```python
import functools
import math

import jax
import jax.numpy as jnp
from jax import lax
from jax.experimental import pallas as pl
from jax.experimental.pallas import tpu as pltpu
from jax.sharding import PartitionSpec as P

CAP = 192
UNROLL = 32
FLOOR = -1e30
F32 = jnp.float32
BF16 = jnp.bfloat16
NT = (((1,), (1,)), ((), ()))


def dot(a, b):
    return jnp.dot(a, b, preferred_element_type=F32)


def dot_nt(a, b):
    return lax.dot_general(a, b, NT, preferred_element_type=F32)


def iota(shape, dim):
    return lax.broadcasted_iota(jnp.int32, shape, dim)


def kernel(
    q_hbm, k_hbm, v_hbm, rk_hbm, rv_hbm, ids_hbm, cnt_hbm, w_hbm,
    out_ref,
    q_v, k_v, v_v, rk_v, rv_v, ids_v, w_v, cnt_s, slot_v, slot_s,
    flip, q32, qh_v, score_v, acc_v, summed_v, mg_v, lg_v, seg_v, tmap_v, base_v,
    msum_v, lsum_v, stat_v, send_v, recv_v, piece_v, att_v, psend_v, precv_v,
    in_sem, slot_sem, rs_s, rs_r, ag_s, ag_r, pj_s, pj_r,
):
    seq = lax.axis_index("seq")
    kvh = lax.axis_index("kvh")
    sy, sx = seq // 4, seq % 4
    scale = 1.0 / math.sqrt(128)

    def seq_at(dy, dx):
        return lax.rem(sy + dy + 4, 4) * 4 + lax.rem(sx + dx + 4, 4)

    shifts = [(dy, dx) for dy in range(4) for dx in range(4) if dy or dx]

    barrier = pltpu.get_barrier_semaphore()
    for dy, dx in shifts:
        pl.semaphore_signal(
            barrier, inc=1, device_id={"seq": seq_at(dy, dx)}, device_id_type=pl.DeviceIdType.MESH
        )
    for e in range(1, 8):
        pl.semaphore_signal(
            barrier, inc=1, device_id={"kvh": lax.rem(kvh + e, 8)}, device_id_type=pl.DeviceIdType.MESH
        )

    loads = [
        pltpu.make_async_copy(src, dst, in_sem.at[i])
        for i, (src, dst) in enumerate(
            [
                (ids_hbm, ids_v), (cnt_hbm, cnt_s), (q_hbm, q_v), (rk_hbm, rk_v),
                (rv_hbm, rv_v), (k_hbm, k_v), (v_hbm, v_v), (w_hbm, w_v),
            ]
        )
    ]
    for load in loads:
        load.start()
    l_ids, l_cnt, l_q, l_rk, l_rv, l_k, l_v, l_w = loads

    flip[...] = jnp.zeros_like(flip)
    l_ids.wait()
    flip[0:16, 0:64] = ids_v[...].astype(F32)
    ids = flip[...].T[0:64, :]
    first_id = (seq * 128).astype(F32)
    local = (ids >= first_id) & (ids < first_id + 128.0) & (iota((64, 128), 1) < 16)
    block = ids - first_id
    hit = jnp.where(local, 1.0, 0.0).astype(BF16)
    ones = jnp.ones((128, 128), BF16)
    above = jnp.where(iota((128, 128), 0) < iota((128, 128), 1), 1.0, 0.0).astype(BF16)
    below = jnp.where(iota((64, 64), 1) < iota((64, 64), 0), 1.0, 0.0).astype(BF16)
    base = dot(dot(below, hit).astype(BF16), ones)
    count = dot(hit, ones)
    rank = jnp.where(local, base + dot(hit, above), -1.0)
    slots = iota((64, 256), 1).astype(F32)
    base2 = jnp.concatenate([base, base], axis=1)
    count2 = jnp.concatenate([count, count], axis=1)
    tmap = jnp.where((slots >= base2) & (slots < base2 + count2), 1.0, 0.0)
    first = jnp.where((slots == base2) & (count2 > 0.0), 1.0, 0.0)
    chosen = jnp.zeros((64, 256), F32)
    for s in range(16):
        chosen += jnp.where(rank[:, s : s + 1] == slots, block[:, s : s + 1], 0.0)
    slot_block = jnp.sum(chosen, axis=0, keepdims=True)
    slot_token = jnp.sum(tmap * iota((64, 256), 0).astype(F32), axis=0, keepdims=True)
    slot_live = jnp.sum(tmap, axis=0, keepdims=True)
    seg_v[...] = jnp.broadcast_to(jnp.where(slot_live > 0.0, slot_token, -1.0), (8, 256))
    slot_v[...] = jnp.where(
        iota((8, 256), 0) == 0, slot_token.astype(jnp.int32) & 63, slot_block.astype(jnp.int32) & 127
    )
    tmap_v[0] = tmap.astype(BF16)
    tmap_v[1] = first.astype(BF16)
    base_v[...] = count
    to_smem = pltpu.make_async_copy(slot_v, slot_s, slot_sem)
    to_smem.start()

    l_q.wait()
    q32[0:512, :] = q_v[...].astype(F32).reshape(512, 128)
    for h in range(8):
        qh_v[h * 64 : h * 64 + 64, :] = q32[pl.ds(h, 64, stride=8), :].astype(BF16)
    l_rk.wait()
    l_rv.wait()
    msum_v[...] = jnp.zeros_like(msum_v)
    for c in range(4):
        s = dot_nt(qh_v[c * 128 : c * 128 + 128, :], rk_v[...]) * scale
        m = jnp.max(s, axis=1, keepdims=True).astype(BF16).astype(F32)
        p = jnp.exp(s - m)
        l = jnp.sum(p, axis=1, keepdims=True)
        a = dot(p.astype(BF16), rv_v[...])
        summed_v[c * 128 : c * 128 + 128, :] = a
        for e in range(2):
            h = 2 * c + e
            msum_v[0:64, h : h + 1] = m[e * 64 : e * 64 + 64]
            lsum_v[:, h : h + 1] = l[e * 64 : e * 64 + 64]

    lane = iota((8, 128), 1)
    l_cnt.wait()
    to_smem.wait()
    l_k.wait()

    def score(g, carry):
        for half in range(UNROLL // 16):
            top = jnp.zeros((8, 128), F32)
            for u in range(16):
                j = g * UNROLL + half * 16 + u
                blk = slot_s[1, j]
                s = dot_nt(q_v[slot_s[0, j]], k_v[blk]) * scale
                s = jnp.where(lane < cnt_s[blk], s, FLOOR)
                score_v[j] = s
                top = jnp.where(lane == u, jnp.max(s, axis=1, keepdims=True), top)
            mg_v[g * (UNROLL // 16) + half] = top
        return carry

    lax.fori_loop(0, CAP // UNROLL, score, 0)

    def gathered(ref):
        sides = []
        for side in range(2):
            found = jnp.zeros((8, 128), F32)
            for i in range(8):
                g = side * 8 + i
                if g < CAP // 16:
                    part = ref[g] if i == 0 else pltpu.roll(ref[g], i * 16, 1)
                    found = jnp.where((lane >= i * 16) & (lane < i * 16 + 16), part, found)
            sides.append(found)
        return jnp.concatenate(sides, axis=1)

    top = gathered(mg_v).astype(BF16).astype(F32)
    token = seg_v[...]
    for back in (False, True):
        for k in (1, 2, 4, 8):
            by = 256 - k if back else k
            same = pltpu.roll(token, by, 1) == token
            top = jnp.maximum(top, jnp.where(same, pltpu.roll(top, by, 1), FLOOR))
    tmap_b, first_b = tmap_v[0], tmap_v[1]
    msum = msum_v[...]
    sum_top = dot(msum.T[0:8, 0:64].astype(BF16), tmap_b)
    top = jnp.maximum(top, sum_top)
    for g in range(CAP // 16):
        part = top[:, (g // 8) * 128 : (g // 8) * 128 + 128]
        mg_v[g] = part if g % 8 == 0 else pltpu.roll(part, 128 - (g % 8) * 16, 1)

    l_v.wait()

    def weigh(g, carry):
        for half in range(UNROLL // 16):
            i = g * (UNROLL // 16) + half
            tops = mg_v[i]
            total = jnp.zeros((8, 128), F32)
            for u in range(16):
                j = g * UNROLL + half * 16 + u
                p = jnp.exp(score_v[j] - tops[:, u : u + 1])
                total = jnp.where(lane == u, jnp.sum(p, axis=1, keepdims=True), total)
                acc_v[pl.ds(j, 8, stride=CAP), :] = dot(p.astype(BF16), v_v[slot_s[1, j]])
            lg_v[i] = total
        return carry

    lax.fori_loop(0, CAP // UNROLL, weigh, 0)

    total = gathered(lg_v)
    total_hi = total.astype(BF16)
    total_lo = (total - total_hi.astype(F32)).astype(BF16)
    sums = dot_nt(tmap_b, total_hi) + dot_nt(tmap_b, total_lo)
    sum_m = msum[0:64, 0:8]
    high = jnp.where(base_v[:, 0:8] > 0.0, dot_nt(first_b, top.astype(BF16)), sum_m)
    factor = jnp.exp(sum_m - high)
    sums = sums + lsum_v[:, 0:8] * factor
    sums_hi = sums.astype(BF16).astype(F32)
    stat_v[...] = jnp.zeros_like(stat_v)
    stat_v[:, 0:8] = high
    stat_v[:, 8:16] = sums_hi
    stat_v[:, 16:24] = sums - sums_hi
    stat = stat_v[...].astype(BF16)
    for o in range(16):
        t = o % 4
        send_v[o, 2] = stat[t * 16 : t * 16 + 16]
    tmap_c = tmap_b[:, 0:CAP]
    for h in range(8):
        a = dot(tmap_c, acc_v[h * CAP : h * CAP + CAP, :].astype(BF16))
        a = a + summed_v[h * 64 : h * 64 + 64, :] * factor[:, h : h + 1]
        a = a.astype(BF16)
        for t in range(4):
            send_v[(h // 2) * 4 + t, h % 2] = a[t * 16 : t * 16 + 16]

    pl.semaphore_wait(barrier, 22)

    def remote(src, dst, send_sem, recv_sem, where):
        return pltpu.make_async_remote_copy(
            src_ref=src, dst_ref=dst, send_sem=send_sem, recv_sem=recv_sem,
            device_id=where, device_id_type=pl.DeviceIdType.MESH,
        )

    order = sorted(shifts, key=lambda d: -(min(d[0], 4 - d[0]) + min(d[1], 4 - d[1])))
    pushes = []
    for dy, dx in order:
        d = dy * 4 + dx
        peer = seq_at(dy, dx)
        pushes.append(
            remote(send_v.at[peer], recv_v.at[d], rs_s.at[d], rs_r.at[d], {"seq": peer})
        )
        pushes[-1].start()
    recv_v[0] = send_v[seq]
    for push in pushes:
        push.wait_recv()
    stats = [recv_v[d, 2].astype(F32) for d in range(16)]
    high = functools.reduce(jnp.maximum, stats)
    factors = [jnp.exp(x - high) for x in stats]
    whole = sum(
        f * (pltpu.roll(x, 120, 1) + pltpu.roll(x, 112, 1)) for f, x in zip(factors, stats)
    )
    mine = 2 * (seq // 4)
    column = iota((16, 128), 1)
    heads = [jnp.zeros((16, 128), F32) for _ in range(2)]
    for d in range(16):
        share = factors[d] / whole
        for e in range(2):
            g = jnp.sum(jnp.where(column == mine + e, share, 0.0), axis=1, keepdims=True)
            heads[e] = heads[e] + recv_v[d, e].astype(F32) * g
    for e in range(2):
        piece_v[e] = heads[e].astype(BF16)

    def place(o):
        return att_v.at[pl.ds(2 * (o // 4), 2), pl.ds(pl.multiple_of(16 * (o % 4), 16), 16), :]

    spreads = []
    for dy, dx in order:
        d = dy * 4 + dx
        peer = seq_at(dy, dx)
        spread = remote(piece_v, place(seq), ag_s.at[d], ag_r.at[d], {"seq": peer})
        spread.start()
        spreads.append((dy, dx, spread))
    place(seq)[...] = piece_v[...]
    for push in pushes:
        push.wait_send()
    l_w.wait()
    for dy, dx, spread in spreads:
        d = dy * 4 + dx
        source = seq_at(-dy, -dx)
        remote(piece_v, place(source), ag_s.at[d], ag_r.at[d], {"seq": source}).wait_recv()

    terms = dot(att_v[0], w_v[0:128, :])
    for h in range(1, 8):
        terms += dot(att_v[h], w_v[h * 128 : h * 128 + 128, :])
    for e in range(8):
        psend_v[e] = terms[e * 8 : e * 8 + 8, :].astype(BF16)
    hands = []
    for e in (4, 5, 3, 6, 2, 7, 1):
        peer = lax.rem(kvh + e, 8)
        hand = remote(psend_v.at[peer], precv_v.at[e], pj_s.at[e], pj_r.at[e], {"kvh": peer})
        hand.start()
        hands.append(hand)
    for _, _, spread in spreads:
        spread.wait_send()
    result = psend_v[kvh].astype(F32)
    for hand in hands:
        hand.wait_recv()
    for e in range(1, 8):
        result = result + precv_v[e].astype(F32)
    out_ref[...] = result.astype(BF16)
    for hand in hands:
        hand.wait_send()


def on_device(queries, keys, values, rep_keys, rep_values, block_ids, block_counts, out_weight):
    vmem, smem, dma = pltpu.VMEM, pltpu.SMEM, pltpu.SemaphoreType.DMA
    any_spec = pl.BlockSpec(memory_space=pl.ANY)
    return pl.pallas_call(
        kernel,
        out_shape=jax.ShapeDtypeStruct((8, 512), BF16),
        in_specs=[any_spec] * 8,
        out_specs=pl.BlockSpec(memory_space=pltpu.VMEM),
        scratch_shapes=[
            vmem((64, 8, 128), BF16), vmem((128, 128, 128), BF16), vmem((128, 128, 128), BF16),
            vmem((512, 128), BF16), vmem((512, 128), BF16), vmem((16, 64), jnp.int32),
            vmem((1024, 512), BF16), smem((128,), jnp.int32), vmem((8, 256), jnp.int32),
            smem((8, 256), jnp.int32),
            vmem((128, 128), F32), vmem((520, 128), F32), vmem((512, 128), BF16),
            vmem((CAP, 8, 128), F32), vmem((9 * CAP, 128), F32), vmem((512, 128), F32),
            vmem((CAP // 16, 8, 128), F32), vmem((CAP // 16, 8, 128), F32), vmem((8, 256), F32),
            vmem((2, 64, 256), BF16), vmem((64, 128), F32),
            vmem((128, 128), F32), vmem((64, 128), F32), vmem((64, 128), F32),
            vmem((16, 3, 16, 128), BF16), vmem((16, 3, 16, 128), BF16), vmem((2, 16, 128), BF16),
            vmem((8, 64, 128), BF16), vmem((8, 8, 512), BF16), vmem((8, 8, 512), BF16),
            dma((8,)), dma, dma((16,)), dma((16,)), dma((16,)), dma((16,)), dma((8,)), dma((8,)),
        ],
        compiler_params=pltpu.CompilerParams(collective_id=0, has_side_effects=True),
        name="decode",
    )(
        queries,
        keys.reshape(keys.shape[0], keys.shape[2], keys.shape[3]),
        values.reshape(values.shape[0], values.shape[2], values.shape[3]),
        rep_keys.reshape(-1, rep_keys.shape[3]),
        rep_values.reshape(-1, rep_values.shape[3]),
        jnp.transpose(block_ids, (1, 2, 0)).reshape(block_ids.shape[2], block_ids.shape[0]),
        block_counts,
        out_weight,
    )


def solution(mesh):
    in_specs = (
        P(None, "kvh", None),
        P("seq", "kvh", None, None),
        P("seq", "kvh", None, None),
        P("seq", "kvh", None, None),
        P("seq", "kvh", None, None),
        P(None, "kvh", None),
        P("seq"),
        P("kvh", "seq"),
    )
    return jax.shard_map(
        on_device, mesh=mesh, in_specs=in_specs, out_specs=P("kvh", "seq"), check_vma=False
    )
```

time: 84 us -> 38.2 us (0.45)
  blocking collectives: 38.5 us -> 0 us
  Pallas kernels: 0 us -> 36.7 us
  local copies, waits for them, and re-layouts: 29.6 us -> 1.3 us
  matrix products: 11.5 us -> 0 us
  other arithmetic: 3.6 us -> 0 us
    pallas_call x0 -> x1, Pallas kernels: none -> 36.7 us  [on_device(): pl.pallas_call(kernel, out_shape=jax.ShapeDtypeStruct((8, 512), BF16), in...]
    gather x5 -> x0, local copies, waits for them, and re-layouts: 25.7 us -> none  [the longest x1 10.5 us: on_device(): tile_keys = keys[slot_block, head_pos[:, None]]]
    all_gather x2 -> x0, blocking collectives: 23 us -> none  [collected_together(): both, at, found = (lax.all_gather(jnp.concatenate(lines), axis), 0, {})]
    all_to_all x1 -> x0, blocking collectives: 15.5 us -> none  [sum_at_owner(): lax.all_to_all(in_blocks(value, dim, devices), axis, 0, 0, tiled=True)]
    dot_general x7 -> x0, matrix products: 11.5 us -> none  [the longest x1 5.56 us: chosen_stats(): jnp.einsum('kjgd,kjtd->kjgt', slot_query, tile_keys, preferred_element_ty...]
    reduce_sum x3 -> x0, other arithmetic: 1.53 us -> none  [the longest x1 0.61 us: sum_at_owner(): return jnp.sum(parts.astype(jnp.float32), axis=0)]
    convert_element_type x15 -> x0, local copies, waits for them, and re-layouts: 1.16 us -> none  [the longest x12 0.85 us: combined_by_axis(): part[k].astype(own.dtype)]
where the time goes in v1:
time: 38.2 us; the launch traced here: 38 us
  Pallas kernels  36.7 us (96%)
  local copies, waits for them, and re-layouts  1.3 us (3%)
    pallas_call x1, Pallas kernels, on_device(): pl.pallas_call(kernel, out_shape=jax.ShapeDtypeStruct((8, 512), BF16), in...  36.7 us
    unnamed x1, local copies, waits for them, and re-layouts  1.3 us

profile of v1, /device:TPU:1, one launch (start us, length us, event | category | flops | bytes accessed | tf_op | source)
XLA Modules:
  0.0 38.0 jit_solution(5182569493140397009)
XLA Ops:
  0.0 36.7 %decode.1 = bf16[8,512]{1,0:T(8,128)(2,1)} custom-call(bf16[64,8,128]{2,1,0:T(8,128)(2,1)} %q_hbm.1, bf16[128,128,128]{2,1,0:T(8,128)(2,1)} %bitcast.7, bf16[128,128,128]{2,1,0:T(8,128)(2,1)} %bitcast.8, bf16[512,128]{1,0:T(8,128)(2,1)} %bitcast.9, bf16[512,128]{1,0:T(8,128)(2,1)} %bitcast.10, s32[16,64]{1,0:T(8,128)} %bitcast.11, s32[128]{0:T(128)} %cnt_hbm.1, ...), custom_call_target="tpu_custom_call" | custom-call | tf_op jit(solution)/shard_map/decode/pallas_call | solution.py:297
  36.7 1.3 %copy.10 = bf16[8,512]{1,0:T(8,128)(2,1)} copy(bf16[8,512]{1,0:T(8,128)(2,1)} %decode.1) | data formatting | bytes 16384

commit v2 on v1

--- a/solution.py
+++ b/solution.py
@@ -9,7 +9,8 @@
 from jax.sharding import PartitionSpec as P
 
 CAP = 192
-UNROLL = 32
+UNROLL = 192
+STRIDE = 196
 FLOOR = -1e30
 F32 = jnp.float32
 BF16 = jnp.bfloat16
@@ -32,7 +33,7 @@
     q_hbm, k_hbm, v_hbm, rk_hbm, rv_hbm, ids_hbm, cnt_hbm, w_hbm,
     out_ref,
     q_v, k_v, v_v, rk_v, rv_v, ids_v, w_v, cnt_s, slot_v, slot_s,
-    flip, q32, qh_v, score_v, acc_v, summed_v, mg_v, lg_v, seg_v, tmap_v, base_v,
+    flip, q3, q32, qh_v, score_v, acc_v, summed_v, mg_v, lg_v, seg_v, tmap_v, base_v,
     msum_v, lsum_v, stat_v, send_v, recv_v, piece_v, att_v, psend_v, precv_v,
     in_sem, slot_sem, rs_s, rs_r, ag_s, ag_r, pj_s, pj_r,
 ):
@@ -70,7 +71,8 @@
     l_ids, l_cnt, l_q, l_rk, l_rv, l_k, l_v, l_w = loads
 
     flip[...] = jnp.zeros_like(flip)
-    l_ids.wait()
+    with jax.named_scope("wait_ids"):
+        l_ids.wait()
     flip[0:16, 0:64] = ids_v[...].astype(F32)
     ids = flip[...].T[0:64, :]
     first_id = (seq * 128).astype(F32)
@@ -104,12 +106,16 @@
     to_smem = pltpu.make_async_copy(slot_v, slot_s, slot_sem)
     to_smem.start()
 
-    l_q.wait()
-    q32[0:512, :] = q_v[...].astype(F32).reshape(512, 128)
+    with jax.named_scope("wait_q"):
+        l_q.wait()
+    wide = q_v[...].astype(F32)
+    q3[...] = wide
+    q32[0:512, :] = wide.reshape(512, 128)
     for h in range(8):
         qh_v[h * 64 : h * 64 + 64, :] = q32[pl.ds(h, 64, stride=8), :].astype(BF16)
-    l_rk.wait()
-    l_rv.wait()
+    with jax.named_scope("wait_rep"):
+        l_rk.wait()
+        l_rv.wait()
     msum_v[...] = jnp.zeros_like(msum_v)
     for c in range(4):
         s = dot_nt(qh_v[c * 128 : c * 128 + 128, :], rk_v[...]) * scale
@@ -124,24 +130,44 @@
             lsum_v[:, h : h + 1] = l[e * 64 : e * 64 + 64]
 
     lane = iota((8, 128), 1)
-    l_cnt.wait()
-    to_smem.wait()
-    l_k.wait()
+    with jax.named_scope("wait_k"):
+        l_cnt.wait()
+        to_smem.wait()
+        l_k.wait()
+
+    empty = jnp.zeros((8, 128), F32)
+
+    def beside(a, b):
+        return jnp.concatenate([a, b], axis=1)
+
+    def four(a, b, c, d):
+        rows = [beside(a, empty), beside(empty, b), beside(c, empty), beside(empty, d)]
+        return jnp.concatenate(rows, axis=0).astype(BF16)
+
+    def apart(r):
+        return r[0:8, 0:128], r[8:16, 0:128], r[16:24, 128:256], r[24:32, 128:256]
+
+    def query(j):
+        return q3[slot_s[0, j]]
 
     def score(g, carry):
         for half in range(UNROLL // 16):
             top = jnp.zeros((8, 128), F32)
-            for u in range(16):
+            for u in range(0, 16, 4):
                 j = g * UNROLL + half * 16 + u
-                blk = slot_s[1, j]
-                s = dot_nt(q_v[slot_s[0, j]], k_v[blk]) * scale
-                s = jnp.where(lane < cnt_s[blk], s, FLOOR)
-                score_v[j] = s
-                top = jnp.where(lane == u, jnp.max(s, axis=1, keepdims=True), top)
+                blk = [slot_s[1, j + i] for i in range(4)]
+                tile = [k_v[blk[i]] for i in range(4)]
+                tile = jnp.concatenate([beside(tile[0], tile[1]), beside(tile[2], tile[3])], axis=0)
+                found = apart(dot_nt(four(*[query(j + i) for i in range(4)]), tile))
+                for i in range(4):
+                    s = jnp.where(lane < cnt_s[blk[i]], found[i] * scale, FLOOR)
+                    score_v[j + i] = s
+                    top = jnp.where(lane == u + i, jnp.max(s, axis=1, keepdims=True), top)
             mg_v[g * (UNROLL // 16) + half] = top
         return carry
 
-    lax.fori_loop(0, CAP // UNROLL, score, 0)
+    with jax.named_scope("score"):
+        lax.fori_loop(0, CAP // UNROLL, score, 0)
 
     def gathered(ref):
         sides = []
@@ -170,22 +196,31 @@
         part = top[:, (g // 8) * 128 : (g // 8) * 128 + 128]
         mg_v[g] = part if g % 8 == 0 else pltpu.roll(part, 128 - (g % 8) * 16, 1)
 
-    l_v.wait()
+    with jax.named_scope("wait_v"):
+        l_v.wait()
 
     def weigh(g, carry):
         for half in range(UNROLL // 16):
-            i = g * (UNROLL // 16) + half
-            tops = mg_v[i]
+            at = g * (UNROLL // 16) + half
+            tops = mg_v[at]
             total = jnp.zeros((8, 128), F32)
-            for u in range(16):
+            for u in range(0, 16, 4):
                 j = g * UNROLL + half * 16 + u
-                p = jnp.exp(score_v[j] - tops[:, u : u + 1])
-                total = jnp.where(lane == u, jnp.sum(p, axis=1, keepdims=True), total)
-                acc_v[pl.ds(j, 8, stride=CAP), :] = dot(p.astype(BF16), v_v[slot_s[1, j]])
-            lg_v[i] = total
+                ps = []
+                for i in range(4):
+                    p = jnp.exp(score_v[j + i] - tops[:, u + i : u + i + 1])
+                    total = jnp.where(lane == u + i, jnp.sum(p, axis=1, keepdims=True), total)
+                    ps.append(p)
+                tile = [v_v[slot_s[1, j + i]] for i in range(4)]
+                tile = jnp.concatenate([beside(tile[0], tile[2]), beside(tile[1], tile[3])], axis=0)
+                found = apart(dot(four(*ps), tile))
+                for i in range(4):
+                    acc_v[pl.ds(j + i, 8, stride=STRIDE), :] = found[i]
+            lg_v[at] = total
         return carry
 
-    lax.fori_loop(0, CAP // UNROLL, weigh, 0)
+    with jax.named_scope("weigh"):
+        lax.fori_loop(0, CAP // UNROLL, weigh, 0)
 
     total = gathered(lg_v)
     total_hi = total.astype(BF16)
@@ -206,13 +241,14 @@
         send_v[o, 2] = stat[t * 16 : t * 16 + 16]
     tmap_c = tmap_b[:, 0:CAP]
     for h in range(8):
-        a = dot(tmap_c, acc_v[h * CAP : h * CAP + CAP, :].astype(BF16))
+        a = dot(tmap_c, acc_v[h * STRIDE : h * STRIDE + CAP, :].astype(BF16))
         a = a + summed_v[h * 64 : h * 64 + 64, :] * factor[:, h : h + 1]
         a = a.astype(BF16)
         for t in range(4):
             send_v[(h // 2) * 4 + t, h % 2] = a[t * 16 : t * 16 + 16]
 
-    pl.semaphore_wait(barrier, 22)
+    with jax.named_scope("barrier"):
+        pl.semaphore_wait(barrier, 22)
 
     def remote(src, dst, send_sem, recv_sem, where):
         return pltpu.make_async_remote_copy(
@@ -230,8 +266,9 @@
         )
         pushes[-1].start()
     recv_v[0] = send_v[seq]
-    for push in pushes:
-        push.wait_recv()
+    with jax.named_scope("rs_recv"):
+        for push in pushes:
+            push.wait_recv()
     stats = [recv_v[d, 2].astype(F32) for d in range(16)]
     high = functools.reduce(jnp.maximum, stats)
     factors = [jnp.exp(x - high) for x in stats]
@@ -260,13 +297,15 @@
         spread.start()
         spreads.append((dy, dx, spread))
     place(seq)[...] = piece_v[...]
-    for push in pushes:
-        push.wait_send()
-    l_w.wait()
-    for dy, dx, spread in spreads:
-        d = dy * 4 + dx
-        source = seq_at(-dy, -dx)
-        remote(piece_v, place(source), ag_s.at[d], ag_r.at[d], {"seq": source}).wait_recv()
+    with jax.named_scope("ag_wait_send"):
+        for push in pushes:
+            push.wait_send()
+        l_w.wait()
+    with jax.named_scope("ag_recv"):
+        for dy, dx, spread in spreads:
+            d = dy * 4 + dx
+            source = seq_at(-dy, -dx)
+            remote(piece_v, place(source), ag_s.at[d], ag_r.at[d], {"seq": source}).wait_recv()
 
     terms = dot(att_v[0], w_v[0:128, :])
     for h in range(1, 8):
@@ -282,13 +321,15 @@
     for _, _, spread in spreads:
         spread.wait_send()
     result = psend_v[kvh].astype(F32)
-    for hand in hands:
-        hand.wait_recv()
+    with jax.named_scope("pj_recv"):
+        for hand in hands:
+            hand.wait_recv()
     for e in range(1, 8):
         result = result + precv_v[e].astype(F32)
     out_ref[...] = result.astype(BF16)
-    for hand in hands:
-        hand.wait_send()
+    with jax.named_scope("pj_send"):
+        for hand in hands:
+            hand.wait_send()
 
 
 def on_device(queries, keys, values, rep_keys, rep_values, block_ids, block_counts, out_weight):
@@ -304,8 +345,8 @@
             vmem((512, 128), BF16), vmem((512, 128), BF16), vmem((16, 64), jnp.int32),
             vmem((1024, 512), BF16), smem((128,), jnp.int32), vmem((8, 256), jnp.int32),
             smem((8, 256), jnp.int32),
-            vmem((128, 128), F32), vmem((520, 128), F32), vmem((512, 128), BF16),
-            vmem((CAP, 8, 128), F32), vmem((9 * CAP, 128), F32), vmem((512, 128), F32),
+            vmem((128, 128), F32), vmem((64, 8, 128), F32), vmem((520, 128), F32), vmem((512, 128), BF16),
+            vmem((CAP, 8, 128), F32), vmem((9 * STRIDE, 128), F32), vmem((512, 128), F32),
             vmem((CAP // 16, 8, 128), F32), vmem((CAP // 16, 8, 128), F32), vmem((8, 256), F32),
             vmem((2, 64, 256), BF16), vmem((64, 128), F32),
             vmem((128, 128), F32), vmem((64, 128), F32), vmem((64, 128), F32),

time: 38.2 us -> 29.8 us (0.78)
  Pallas kernels: 36.7 us -> 28.3 us
    pallas_call x1, Pallas kernels: 36.7 us -> 28.3 us  [on_device(): pl.pallas_call(kernel, out_shape=jax.ShapeDtypeStruct((8, 512), BF16), in...]
where the time goes in v2:
time: 29.8 us; the launch traced here: 29.6 us
  Pallas kernels  28.3 us (95%)
  local copies, waits for them, and re-layouts  1.3 us (4%)
    pallas_call x1, Pallas kernels, on_device(): pl.pallas_call(kernel, out_shape=jax.ShapeDtypeStruct((8, 512), BF16), in...  28.3 us
    unnamed x1, local copies, waits for them, and re-layouts  1.3 us

profile of v2, /device:TPU:1, one launch (start us, length us, event | category | flops | bytes accessed | tf_op | source)
XLA Modules:
  0.0 29.6 jit_solution(396291049373051121)
XLA Ops:
  0.0 28.3 %decode.1 = bf16[8,512]{1,0:T(8,128)(2,1)} custom-call(bf16[64,8,128]{2,1,0:T(8,128)(2,1)} %q_hbm.1, bf16[128,128,128]{2,1,0:T(8,128)(2,1)} %bitcast.7, bf16[128,128,128]{2,1,0:T(8,128)(2,1)} %bitcast.8, bf16[512,128]{1,0:T(8,128)(2,1)} %bitcast.9, bf16[512,128]{1,0:T(8,128)(2,1)} %bitcast.10, s32[16,64]{1,0:T(8,128)} %bitcast.11, s32[128]{0:T(128)} %cnt_hbm.1, ...), custom_call_target="tpu_custom_call" | custom-call | tf_op jit(solution)/shard_map/decode/pallas_call | solution.py:338
  28.3 1.3 %copy.10 = bf16[8,512]{1,0:T(8,128)(2,1)} copy(bf16[8,512]{1,0:T(8,128)(2,1)} %decode.1) | data formatting | bytes 16384

commit v3 on v2

v3 whole, which is shorter than its diff:
```python
import functools
import math

import jax
import jax.numpy as jnp
from jax import lax
from jax.experimental import pallas as pl
from jax.experimental.pallas import tpu as pltpu
from jax.sharding import PartitionSpec as P

CAP = 192
STRIDE = 196
FLOOR = -1e30
F32 = jnp.float32
BF16 = jnp.bfloat16
NT = (((1,), (1,)), ((), ()))


def dot(a, b):
    return jnp.dot(a, b, preferred_element_type=F32)


def dot_nt(a, b):
    return lax.dot_general(a, b, NT, preferred_element_type=F32)


def iota(shape, dim):
    return lax.broadcasted_iota(jnp.int32, shape, dim)


def kernel(
    q_hbm, k_hbm, v_hbm, rk_hbm, rv_hbm, ids_hbm, cnt_hbm, w_hbm,
    out_ref,
    q_v, k_v, v_v, rk_v, rv_v, ids_v, w_v, cnt_s, slot_v, slot_s,
    wide_v, q3, q32, qh_v, rs_v, rp_v, weight_v, acc_v, summed_v, seg_v,
    tmap_v, col_v, row_v, cnt_v, send_v, recv_v, zsend_v, zrecv_v, piece_v, att_v, psend_v, precv_v,
    in_sem, slot_sem, rs_s, rs_r, rz_s, rz_r, ag_s, ag_r, pj_s, pj_r,
):
    seq = lax.axis_index("seq")
    kvh = lax.axis_index("kvh")
    sy, sx = seq // 4, seq % 4
    scale = 1.0 / math.sqrt(128)

    def seq_at(dy, dx):
        return lax.rem(sy + dy + 4, 4) * 4 + lax.rem(sx + dx + 4, 4)

    shifts = [(dy, dx) for dy in range(4) for dx in range(4) if dy or dx]

    barrier = pltpu.get_barrier_semaphore()
    loads = [
        pltpu.make_async_copy(src, dst, in_sem.at[i])
        for i, (src, dst) in enumerate(
            [
                (ids_hbm, ids_v), (cnt_hbm, cnt_s), (q_hbm, q_v), (rk_hbm, rk_v),
                (rv_hbm, rv_v), (k_hbm, k_v), (v_hbm, v_v), (w_hbm, w_v),
            ]
        )
    ]
    for load in loads:
        load.start()
    l_ids, l_cnt, l_q, l_rk, l_rv, l_k, l_v, l_w = loads
    for dy, dx in shifts:
        pl.semaphore_signal(
            barrier, inc=1, device_id={"seq": seq_at(dy, dx)}, device_id_type=pl.DeviceIdType.MESH
        )
    for e in range(1, 8):
        pl.semaphore_signal(
            barrier, inc=1, device_id={"kvh": lax.rem(kvh + e, 8)}, device_id_type=pl.DeviceIdType.MESH
        )

    def where_true(cond):
        return jnp.where(cond, 1.0, 0.0).astype(BF16)

    wide_v[...] = jnp.full_like(wide_v, -1.0)
    col_v[...] = jnp.zeros_like(col_v)
    slot_v[...] = jnp.zeros_like(slot_v)
    with jax.named_scope("wait_ids"):
        l_ids.wait()
    wide_v[:, 0:64] = ids_v[...].astype(F32)
    ids = wide_v[...]
    first_id = (seq * 128).astype(F32)
    local = (ids >= first_id) & (ids < first_id + 128.0)
    block = ids - first_id
    hit = where_true(local)
    before = where_true(iota((16, 16), 1) < iota((16, 16), 0))
    counts = dot(jnp.ones((256, 16), BF16), hit)
    earlier = where_true(iota((128, 128), 0) < iota((128, 128), 1))
    rank = dot(counts[0:16].astype(BF16), earlier) + dot(before, hit)
    rank = jnp.where(local, rank, -1.0).astype(jnp.int32)
    high, low = rank >> 4, rank & 15
    digit = iota((16, 128), 0)
    token_at = iota((16, 128), 1).astype(F32)
    blocks, tokens, lows = [], [], []
    for s in range(16):
        same = high[s : s + 1, :] == digit
        blocks.append(jnp.where(same, block[s : s + 1, :], 0.0))
        tokens.append(jnp.where(same, token_at, 0.0))
        lows.append(jnp.where(low[s : s + 1, :] == digit, 1.0, 0.0))
    chosen = [jnp.concatenate(x, axis=1).astype(BF16) for x in (blocks, tokens, lows)]
    slots = dot_nt(chosen[2], jnp.concatenate(chosen[0:2], axis=0)).astype(jnp.int32)
    slot_v[:, 0:32] = slots & jnp.where(iota((16, 32), 1) < 16, 127, 63)
    to_smem = pltpu.make_async_copy(slot_v, slot_s, slot_sem)
    to_smem.start()
    cnt_v[...] = counts[0:8]
    counts = counts.astype(BF16)
    base = dot_nt(where_true(iota((64, 128), 1) < iota((64, 128), 0)), counts)
    count = dot_nt(where_true(iota((64, 128), 1) == iota((64, 128), 0)), counts)
    at = iota((64, 256), 1).astype(F32)
    tmap = jnp.where((at >= base) & (at < base + count), 1.0, 0.0)
    slot_token = jnp.sum(tmap * (iota((64, 256), 0) + 1).astype(F32), axis=0, keepdims=True)
    seg_v[...] = jnp.broadcast_to(slot_token, (8, 256))
    tmap_v[0] = tmap.astype(BF16)
    tmap_v[1] = where_true((at == base) & (count > 0.0))
    tmap_v[2] = where_true(count > 0.0)

    with jax.named_scope("wait_q"):
        l_q.wait()
        l_rk.wait()
        l_rv.wait()
    wide = q_v[...].astype(F32)
    q3[...] = wide
    q32[0:512, :] = wide.reshape(512, 128)
    for h in range(8):
        qh_v[h * 64 : h * 64 + 64, :] = q32[pl.ds(h, 64, stride=8), :].astype(BF16)
    rs_v[...] = dot_nt(qh_v[...], rk_v[...])
    for h in range(8):
        s = rs_v[h * 64 : h * 64 + 64, :] * scale
        m = jnp.max(s, axis=1, keepdims=True)
        p = jnp.exp(s - m)
        rp_v[h * 64 : h * 64 + 64, :] = p.astype(BF16)
        col_v[0:64, h : h + 1] = m
        col_v[0:64, 8 + h : 9 + h] = jnp.sum(p, axis=1, keepdims=True)
    summed_v[...] = dot(rp_v[...], rv_v[...])
    row_v[...] = col_v[...].T[0:16, :]

    lane = iota((8, 128), 1)
    empty = jnp.zeros((8, 128), F32)

    def beside(a, b):
        return jnp.concatenate([a, b], axis=1)

    def four(a, b, c, d):
        rows = [beside(a, empty), beside(empty, b), beside(c, empty), beside(empty, d)]
        return jnp.concatenate(rows, axis=0).astype(BF16)

    def apart(r):
        return r[0:8, 0:128], r[8:16, 0:128], r[16:24, 128:256], r[24:32, 128:256]

    with jax.named_scope("wait_smem"):
        l_cnt.wait()
        to_smem.wait()
    with jax.named_scope("wait_k"):
        l_k.wait()
    tops, totals = [empty, empty], [empty, empty]
    for j in range(0, CAP, 4):
        own = range(4)
        half = j // 128
        blk = [slot_s[j % 16 + i, j // 16] for i in own]
        query = [q3[slot_s[j % 16 + i, 16 + j // 16]] for i in own]
        tile = [k_v[blk[i]] for i in own]
        tile = jnp.concatenate([beside(tile[0], tile[1]), beside(tile[2], tile[3])], axis=0)
        found = apart(dot_nt(four(*query), tile))
        ps = []
        for i in own:
            here = lane == (j + i) % 128
            s = jnp.where(lane < cnt_s[blk[i]], found[i] * scale, FLOOR)
            m = jnp.max(s, axis=1, keepdims=True)
            p = jnp.exp(s - m)
            tops[half] = jnp.where(here, m, tops[half])
            totals[half] = jnp.where(here, jnp.sum(p, axis=1, keepdims=True), totals[half])
            ps.append(p)
        weight_v[j // 4] = four(*ps)
    with jax.named_scope("wait_v"):
        l_v.wait()
    for j in range(0, CAP, 4):
        tile = [v_v[slot_s[j % 16 + i, j // 16]] for i in own]
        tile = jnp.concatenate([beside(tile[0], tile[2]), beside(tile[1], tile[3])], axis=0)
        found = apart(dot(weight_v[j // 4], tile))
        for i in own:
            acc_v[pl.ds(j + i, 8, stride=STRIDE), :] = found[i]

    top, total = beside(*tops), beside(*totals)
    token = seg_v[...]
    most = top
    for back in (False, True):
        for k in (1, 2, 4, 8):
            by = 256 - k if back else k
            same = pltpu.roll(token, by, 1) == token
            most = jnp.maximum(most, jnp.where(same, pltpu.roll(most, by, 1), FLOOR))
    tmap_b, first_b = tmap_v[0], tmap_v[1]
    sum_m, sum_l = row_v[0:8, 0:64], row_v[8:16, 0:64]
    most = jnp.maximum(most, dot(sum_m.astype(BF16), tmap_b)).astype(BF16)
    shrink = jnp.exp(top - most.astype(F32))
    total = total * shrink
    total_hi = total.astype(BF16)
    total_lo = (total - total_hi.astype(F32)).astype(BF16)
    high = jnp.where(
        cnt_v[:, 0:64] > 0.0, dot_nt(most, first_b), sum_m.astype(BF16).astype(F32)
    )
    sums = dot_nt(total_hi, tmap_b) + dot_nt(total_lo, tmap_b) + sum_l * jnp.exp(sum_m - high)
    for y in range(4):
        zsend_v[y, :, 0:64] = high[2 * y : 2 * y + 2]
        zsend_v[y, :, 64:128] = sums[2 * y : 2 * y + 2]
    col_m = col_v[0:64, 0:8]
    high_col = jnp.where(
        tmap_v[2][:, 0:8].astype(F32) > 0.0, dot_nt(first_b, most), col_m.astype(BF16).astype(F32)
    )
    factor = jnp.exp(col_m - high_col)
    tmap_f = tmap_b[:, 0:CAP].astype(F32)
    lane8 = iota((64, 8), 1)
    for h in range(8):
        mine = (tmap_f * shrink[h : h + 1, 0:CAP]).astype(BF16)
        a = dot(mine, acc_v[h * STRIDE : h * STRIDE + CAP, :].astype(BF16))
        keep = jnp.sum(jnp.where(lane8 == h, factor, 0.0), axis=1, keepdims=True)
        a = (a + summed_v[h * 64 : h * 64 + 64, :] * keep).astype(BF16)
        for t in range(4):
            send_v[(h // 2) * 4 + t, h % 2] = a[t * 16 : t * 16 + 16]

    with jax.named_scope("barrier"):
        pl.semaphore_wait(barrier, 22)

    def remote(src, dst, send_sem, recv_sem, where):
        return pltpu.make_async_remote_copy(
            src_ref=src, dst_ref=dst, send_sem=send_sem, recv_sem=recv_sem,
            device_id=where, device_id_type=pl.DeviceIdType.MESH,
        )

    order = sorted(shifts, key=lambda d: -(min(d[0], 4 - d[0]) + min(d[1], 4 - d[1])))
    pushes = []
    for dy, dx in order:
        d = dy * 4 + dx
        peer = seq_at(dy, dx)
        for push in (
            remote(zsend_v.at[peer // 4], zrecv_v.at[d], rz_s.at[d], rz_r.at[d], {"seq": peer}),
            remote(send_v.at[peer], recv_v.at[d], rs_s.at[d], rs_r.at[d], {"seq": peer}),
        ):
            push.start()
            pushes.append(push)
    recv_v[0] = send_v[seq]
    zrecv_v[0] = zsend_v[sy]
    with jax.named_scope("rs_recv"):
        for push in pushes:
            push.wait_recv()
    pick = where_true(iota((16, 128), 1) == iota((16, 128), 0) + 16 * sx)
    heads = []
    for e in range(2):
        z = jnp.concatenate([zrecv_v[d, e : e + 1, :] for d in range(16)], axis=0)
        f = jnp.exp(z - jnp.max(z, axis=0, keepdims=True))
        f = jnp.where(iota((16, 128), 1) < 64, f, 0.0)
        whole = jnp.sum(f * pltpu.roll(z, 64, 1), axis=0, keepdims=True)
        g = jnp.where(iota((16, 128), 1) < 64, f / whole, 0.0)
        g_hi = g.astype(BF16)
        g_lo = (g - g_hi.astype(F32)).astype(BF16)
        share = dot_nt(pick, g_hi) + dot_nt(pick, g_lo)
        found = jnp.zeros((16, 128), F32)
        for d in range(16):
            part = jnp.where(iota((16, 16), 1) == d, share, 0.0)
            found = found + recv_v[d, e].astype(F32) * jnp.sum(part, axis=1, keepdims=True)
        piece_v[e] = found.astype(BF16)

    def place(o):
        return att_v.at[pl.ds(2 * (o // 4), 2), pl.ds(pl.multiple_of(16 * (o % 4), 16), 16), :]

    spreads = {}
    for dy, dx in order:
        d = dy * 4 + dx
        peer = seq_at(dy, dx)
        spreads[dy, dx] = remote(piece_v, place(seq), ag_s.at[d], ag_r.at[d], {"seq": peer})
        spreads[dy, dx].start()
    place(seq)[...] = piece_v[...]
    for push in pushes:
        push.wait_send()
    l_w.wait()

    terms = None
    for dy in (0, 1, 3, 2):
        with jax.named_scope(f"ag_recv{dy}"):
            for dx in range(4):
                if dy or dx:
                    d = dy * 4 + dx
                    source = seq_at(-dy, -dx)
                    remote(
                        piece_v, place(source), ag_s.at[d], ag_r.at[d], {"seq": source}
                    ).wait_recv()
        y = lax.rem(sy - dy + 4, 4)
        for e in range(2):
            term = dot(att_v[2 * y + e], w_v[2 * y + e])
            terms = term if terms is None else terms + term
    for e in range(8):
        psend_v[e] = terms[e * 8 : e * 8 + 8, :].astype(BF16)
    hands = []
    for e in (4, 5, 3, 6, 2, 7, 1):
        peer = lax.rem(kvh + e, 8)
        hand = remote(psend_v.at[peer], precv_v.at[e], pj_s.at[e], pj_r.at[e], {"kvh": peer})
        hand.start()
        hands.append(hand)
    for spread in spreads.values():
        spread.wait_send()
    result = psend_v[kvh].astype(F32)
    with jax.named_scope("pj_recv"):
        for hand in hands:
            hand.wait_recv()
    for e in range(1, 8):
        result = result + precv_v[e].astype(F32)
    out_ref[...] = result.astype(BF16)
    with jax.named_scope("pj_send"):
        for hand in hands:
            hand.wait_send()


def on_device(queries, keys, values, rep_keys, rep_values, block_ids, block_counts, out_weight):
    vmem, smem, dma = pltpu.VMEM, pltpu.SMEM, pltpu.SemaphoreType.DMA
    any_spec = pl.BlockSpec(memory_space=pltpu.HBM)
    return pl.pallas_call(
        kernel,
        out_shape=jax.ShapeDtypeStruct((8, 512), BF16),
        in_specs=[any_spec] * 8,
        out_specs=pl.BlockSpec(memory_space=pltpu.VMEM),
        scratch_shapes=[
            vmem((64, 8, 128), BF16), vmem((128, 128, 128), BF16), vmem((128, 128, 128), BF16),
            vmem((512, 128), BF16), vmem((512, 128), BF16), vmem((16, 64), jnp.int32),
            vmem((8, 128, 512), BF16), smem((128,), jnp.int32), vmem((16, 128), jnp.int32),
            smem((16, 128), jnp.int32),
            vmem((16, 128), F32), vmem((64, 8, 128), F32), vmem((520, 128), F32),
            vmem((512, 128), BF16), vmem((512, 512), F32), vmem((512, 512), BF16), vmem((CAP // 4, 32, 256), BF16),
            vmem((9 * STRIDE, 128), F32), vmem((512, 128), F32), vmem((8, 256), F32),
            vmem((3, 64, 256), BF16), vmem((128, 128), F32), vmem((16, 128), F32),
            vmem((8, 128), F32),
            vmem((16, 2, 16, 128), BF16), vmem((16, 2, 16, 128), BF16),
            vmem((4, 2, 128), F32), vmem((16, 2, 128), F32), vmem((2, 16, 128), BF16),
            vmem((8, 64, 128), BF16), vmem((8, 8, 512), BF16), vmem((8, 8, 512), BF16),
            dma((8,)), dma, dma((16,)), dma((16,)), dma((16,)), dma((16,)), dma((16,)), dma((16,)),
            dma((8,)), dma((8,)),
        ],
        compiler_params=pltpu.CompilerParams(collective_id=0, has_side_effects=True, vmem_limit_bytes=24 * 1024 * 1024),
        name="decode",
    )(*[pltpu.with_memory_space_constraint(x, pltpu.HBM) for x in (
        queries,
        keys.reshape(keys.shape[0], keys.shape[2], keys.shape[3]),
        values.reshape(values.shape[0], values.shape[2], values.shape[3]),
        rep_keys.reshape(-1, rep_keys.shape[3]),
        rep_values.reshape(-1, rep_values.shape[3]),
        jnp.transpose(block_ids, (1, 2, 0)).reshape(block_ids.shape[2], block_ids.shape[0]),
        block_counts,
        out_weight.reshape(8, 128, out_weight.shape[1]),
    )])


def solution(mesh):
    in_specs = (
        P(None, "kvh", None),
        P("seq", "kvh", None, None),
        P("seq", "kvh", None, None),
        P("seq", "kvh", None, None),
        P("seq", "kvh", None, None),
        P(None, "kvh", None),
        P("seq"),
        P("kvh", "seq"),
    )
    return jax.shard_map(
        on_device, mesh=mesh, in_specs=in_specs, out_specs=P("kvh", "seq"), check_vma=False
    )
```

time: 29.8 us -> 26.7 us (0.90)
  Pallas kernels: 28.3 us -> 25.9 us
  local copies, waits for them, and re-layouts: 1.3 us -> 0.6 us
    pallas_call x1, Pallas kernels: 28.3 us -> 25.9 us  [on_device(): pl.pallas_call(kernel, out_shape=jax.ShapeDtypeStruct((8, 512), BF16), in...]
    unnamed x1, local copies, waits for them, and re-layouts: 1.3 us -> 0.6 us
where the time goes in v3:
time: 26.7 us; the launch traced here: 26.5 us
  Pallas kernels  25.9 us (97%)
  local copies, waits for them, and re-layouts  0.6 us (2%)
    pallas_call x1, Pallas kernels, on_device(): pl.pallas_call(kernel, out_shape=jax.ShapeDtypeStruct((8, 512), BF16), in...  25.9 us
    unnamed x1, local copies, waits for them, and re-layouts  0.6 us

profile of v3, /device:TPU:1, one launch (start us, length us, event | category | flops | bytes accessed | tf_op | source)
XLA Modules:
  0.0 26.5 jit_solution(15813659787564023954)
XLA Ops:
  0.0 25.9 %decode.1 = bf16[8,512]{1,0:T(8,128)(2,1)S(1)} custom-call(bf16[64,8,128]{2,1,0:T(8,128)(2,1)} %q_hbm.1, bf16[128,128,128]{2,1,0:T(8,128)(2,1)} %bitcast.8, bf16[128,128,128]{2,1,0:T(8,128)(2,1)} %bitcast.9, bf16[512,128]{1,0:T(8,128)(2,1)} %bitcast.11, bf16[512,128]{1,0:T(8,128)(2,1)} %bitcast.12, s32[16,64]{1,0:T(8,128)} %bitcast.13, s32[128]{0:T(128)} %cnt_hbm.1, ...), custom_call_target="tpu_custom_call" | custom-call | tf_op jit(solution)/shard_map/decode/pallas_call | solution.py:314
  25.9 0.6 %copy.10 = bf16[8,512]{1,0:T(8,128)(2,1)} copy(bf16[8,512]{1,0:T(8,128)(2,1)S(1)} %decode.1) | data formatting | bytes 16384

commit v4 on v3

--- a/solution.py
+++ b/solution.py
@@ -31,7 +31,7 @@
 def kernel(
     q_hbm, k_hbm, v_hbm, rk_hbm, rv_hbm, ids_hbm, cnt_hbm, w_hbm,
     out_ref,
-    q_v, k_v, v_v, rk_v, rv_v, ids_v, w_v, cnt_s, slot_v, slot_s,
+    small_v, k_v, v_v, ids_v, w_v, cnt_s, slot_v, slot_s,
     wide_v, q3, q32, qh_v, rs_v, rp_v, weight_v, acc_v, summed_v, seg_v,
     tmap_v, col_v, row_v, cnt_v, send_v, recv_v, zsend_v, zrecv_v, piece_v, att_v, psend_v, precv_v,
     in_sem, slot_sem, rs_s, rs_r, rz_s, rz_r, ag_s, ag_r, pj_s, pj_r,
@@ -49,16 +49,19 @@
     barrier = pltpu.get_barrier_semaphore()
     loads = [
         pltpu.make_async_copy(src, dst, in_sem.at[i])
-        for i, (src, dst) in enumerate(
-            [
-                (ids_hbm, ids_v), (cnt_hbm, cnt_s), (q_hbm, q_v), (rk_hbm, rk_v),
-                (rv_hbm, rv_v), (k_hbm, k_v), (v_hbm, v_v), (w_hbm, w_v),
-            ]
-        )
+        for src, dst, i in [
+            (ids_hbm, ids_v, 0), (cnt_hbm, cnt_s, 1), (q_hbm, small_v.at[0], 2),
+            (rk_hbm, small_v.at[1], 2), (rv_hbm, small_v.at[2], 2), (k_hbm, k_v, 3),
+            (v_hbm, v_v, 4), (w_hbm, w_v, 5),
+        ]
     ]
     for load in loads:
         load.start()
-    l_ids, l_cnt, l_q, l_rk, l_rv, l_k, l_v, l_w = loads
+    l_ids, l_cnt, _, _, _, l_k, l_v, l_w = loads
+
+    def wait_for(like, sem):
+        pltpu.make_async_copy(like, like, sem).wait()
+
     for dy, dx in shifts:
         pl.semaphore_signal(
             barrier, inc=1, device_id={"seq": seq_at(dy, dx)}, device_id_type=pl.DeviceIdType.MESH
@@ -114,15 +117,13 @@
     tmap_v[2] = where_true(count > 0.0)
 
     with jax.named_scope("wait_q"):
-        l_q.wait()
-        l_rk.wait()
-        l_rv.wait()
-    wide = q_v[...].astype(F32)
-    q3[...] = wide
-    q32[0:512, :] = wide.reshape(512, 128)
+        wait_for(small_v, in_sem.at[2])
+    wide = small_v[0].astype(F32)
+    q3[...] = wide.reshape(64, 8, 128)
+    q32[0:512, :] = wide
     for h in range(8):
         qh_v[h * 64 : h * 64 + 64, :] = q32[pl.ds(h, 64, stride=8), :].astype(BF16)
-    rs_v[...] = dot_nt(qh_v[...], rk_v[...])
+    rs_v[...] = dot_nt(qh_v[...], small_v[1])
     for h in range(8):
         s = rs_v[h * 64 : h * 64 + 64, :] * scale
         m = jnp.max(s, axis=1, keepdims=True)
@@ -130,7 +131,7 @@
         rp_v[h * 64 : h * 64 + 64, :] = p.astype(BF16)
         col_v[0:64, h : h + 1] = m
         col_v[0:64, 8 + h : 9 + h] = jnp.sum(p, axis=1, keepdims=True)
-    summed_v[...] = dot(rp_v[...], rv_v[...])
+    summed_v[...] = dot(rp_v[...], small_v[2])
     row_v[...] = col_v[...].T[0:16, :]
 
     lane = iota((8, 128), 1)
@@ -226,21 +227,19 @@
         )
 
     order = sorted(shifts, key=lambda d: -(min(d[0], 4 - d[0]) + min(d[1], 4 - d[1])))
-    pushes = []
     for dy, dx in order:
         d = dy * 4 + dx
         peer = seq_at(dy, dx)
         for push in (
-            remote(zsend_v.at[peer // 4], zrecv_v.at[d], rz_s.at[d], rz_r.at[d], {"seq": peer}),
-            remote(send_v.at[peer], recv_v.at[d], rs_s.at[d], rs_r.at[d], {"seq": peer}),
+            remote(zsend_v.at[peer // 4], zrecv_v.at[d], rz_s, rz_r, {"seq": peer}),
+            remote(send_v.at[peer], recv_v.at[d], rs_s, rs_r, {"seq": peer}),
         ):
             push.start()
-            pushes.append(push)
     recv_v[0] = send_v[seq]
     zrecv_v[0] = zsend_v[sy]
     with jax.named_scope("rs_recv"):
-        for push in pushes:
-            push.wait_recv()
+        wait_for(zrecv_v.at[pl.ds(1, 15)], rz_r)
+        wait_for(recv_v.at[pl.ds(1, 15)], rs_r)
     pick = where_true(iota((16, 128), 1) == iota((16, 128), 0) + 16 * sx)
     heads = []
     for e in range(2):
@@ -261,51 +260,35 @@
     def place(o):
         return att_v.at[pl.ds(2 * (o // 4), 2), pl.ds(pl.multiple_of(16 * (o % 4), 16), 16), :]
 
-    spreads = {}
     for dy, dx in order:
-        d = dy * 4 + dx
-        peer = seq_at(dy, dx)
-        spreads[dy, dx] = remote(piece_v, place(seq), ag_s.at[d], ag_r.at[d], {"seq": peer})
-        spreads[dy, dx].start()
+        remote(piece_v, place(seq), ag_s, ag_r.at[dy], {"seq": seq_at(dy, dx)}).start()
     place(seq)[...] = piece_v[...]
-    for push in pushes:
-        push.wait_send()
+    wait_for(zrecv_v.at[pl.ds(1, 15)], rz_s)
+    wait_for(send_v.at[pl.ds(1, 15)], rs_s)
     l_w.wait()
 
     terms = None
     for dy in (0, 1, 3, 2):
+        y = lax.rem(sy - dy + 4, 4)
         with jax.named_scope(f"ag_recv{dy}"):
-            for dx in range(4):
-                if dy or dx:
-                    d = dy * 4 + dx
-                    source = seq_at(-dy, -dx)
-                    remote(
-                        piece_v, place(source), ag_s.at[d], ag_r.at[d], {"seq": source}
-                    ).wait_recv()
-        y = lax.rem(sy - dy + 4, 4)
+            wait_for(att_v.at[pl.ds(2 * y, 2), pl.ds(0, 64 if dy else 48)], ag_r.at[dy])
         for e in range(2):
             term = dot(att_v[2 * y + e], w_v[2 * y + e])
             terms = term if terms is None else terms + term
     for e in range(8):
         psend_v[e] = terms[e * 8 : e * 8 + 8, :].astype(BF16)
-    hands = []
     for e in (4, 5, 3, 6, 2, 7, 1):
         peer = lax.rem(kvh + e, 8)
-        hand = remote(psend_v.at[peer], precv_v.at[e], pj_s.at[e], pj_r.at[e], {"kvh": peer})
-        hand.start()
-        hands.append(hand)
-    for spread in spreads.values():
-        spread.wait_send()
+        remote(psend_v.at[peer], precv_v.at[e], pj_s, pj_r, {"kvh": peer}).start()
+    wait_for(recv_v.at[pl.ds(1, 15)], ag_s)
     result = psend_v[kvh].astype(F32)
     with jax.named_scope("pj_recv"):
-        for hand in hands:
-            hand.wait_recv()
+        wait_for(precv_v.at[pl.ds(1, 7)], pj_r)
     for e in range(1, 8):
         result = result + precv_v[e].astype(F32)
     out_ref[...] = result.astype(BF16)
     with jax.named_scope("pj_send"):
-        for hand in hands:
-            hand.wait_send()
+        wait_for(psend_v.at[pl.ds(1, 7)], pj_s)
 
 
 def on_device(queries, keys, values, rep_keys, rep_values, block_ids, block_counts, out_weight):
@@ -317,8 +300,8 @@
         in_specs=[any_spec] * 8,
         out_specs=pl.BlockSpec(memory_space=pltpu.VMEM),
         scratch_shapes=[
-            vmem((64, 8, 128), BF16), vmem((128, 128, 128), BF16), vmem((128, 128, 128), BF16),
-            vmem((512, 128), BF16), vmem((512, 128), BF16), vmem((16, 64), jnp.int32),
+            vmem((3, 512, 128), BF16), vmem((128, 128, 128), BF16), vmem((128, 128, 128), BF16),
+            vmem((16, 64), jnp.int32),
             vmem((8, 128, 512), BF16), smem((128,), jnp.int32), vmem((16, 128), jnp.int32),
             smem((16, 128), jnp.int32),
             vmem((16, 128), F32), vmem((64, 8, 128), F32), vmem((520, 128), F32),
@@ -329,13 +312,12 @@
             vmem((16, 2, 16, 128), BF16), vmem((16, 2, 16, 128), BF16),
             vmem((4, 2, 128), F32), vmem((16, 2, 128), F32), vmem((2, 16, 128), BF16),
             vmem((8, 64, 128), BF16), vmem((8, 8, 512), BF16), vmem((8, 8, 512), BF16),
-            dma((8,)), dma, dma((16,)), dma((16,)), dma((16,)), dma((16,)), dma((16,)), dma((16,)),
-            dma((8,)), dma((8,)),
+            dma((6,)), dma, dma, dma, dma, dma, dma, dma((4,)), dma, dma,
         ],
         compiler_params=pltpu.CompilerParams(collective_id=0, has_side_effects=True, vmem_limit_bytes=24 * 1024 * 1024),
         name="decode",
     )(*[pltpu.with_memory_space_constraint(x, pltpu.HBM) for x in (
-        queries,
+        queries.reshape(-1, queries.shape[2]),
         keys.reshape(keys.shape[0], keys.shape[2], keys.shape[3]),
         values.reshape(values.shape[0], values.shape[2], values.shape[3]),
         rep_keys.reshape(-1, rep_keys.shape[3]),

time: 26.7 us -> 25.7 us (0.963)
  Pallas kernels: 25.9 us -> 25 us
    pallas_call x1, Pallas kernels: 25.9 us -> 25 us  [on_device(): pl.pallas_call(kernel, out_shape=jax.ShapeDtypeStruct((8, 512), BF16), in...]
where the time goes in v4:
time: 25.7 us; the launch traced here: 25.6 us
  Pallas kernels  25 us (97%)
  local copies, waits for them, and re-layouts  0.6 us (2%)
    pallas_call x1, Pallas kernels, on_device(): pl.pallas_call(kernel, out_shape=jax.ShapeDtypeStruct((8, 512), BF16), in...  25 us
    unnamed x1, local copies, waits for them, and re-layouts  0.6 us

profile of v4, /device:TPU:1, one launch (start us, length us, event | category | flops | bytes accessed | tf_op | source)
XLA Modules:
  0.0 25.6 jit_solution(7946136860295949452)
XLA Ops:
  0.0 25.0 %decode.1 = bf16[8,512]{1,0:T(8,128)(2,1)S(1)} custom-call(bf16[512,128]{1,0:T(8,128)(2,1)} %bitcast.12, bf16[128,128,128]{2,1,0:T(8,128)(2,1)} %bitcast.9, bf16[128,128,128]{2,1,0:T(8,128)(2,1)} %bitcast.10, bf16[512,128]{1,0:T(8,128)(2,1)} %bitcast.13, bf16[512,128]{1,0:T(8,128)(2,1)} %bitcast.14, s32[16,64]{1,0:T(8,128)} %bitcast.15, s32[128]{0:T(128)} %cnt_hbm.1, ...), custom_call_target="tpu_custom_call" | custom-call | tf_op jit(solution)/shard_map/decode/pallas_call | solution.py:297
  25.0 0.6 %copy.10 = bf16[8,512]{1,0:T(8,128)(2,1)} copy(bf16[8,512]{1,0:T(8,128)(2,1)S(1)} %decode.1) | data formatting | bytes 16384

commit v5 on v4

--- a/solution.py
+++ b/solution.py
@@ -39,6 +39,9 @@
     seq = lax.axis_index("seq")
     kvh = lax.axis_index("kvh")
     sy, sx = seq // 4, seq % 4
+    core = lax.rem(kvh, 2)
+    other = kvh + 1 - 2 * core
+    keeper = kvh + 1 - core
     scale = 1.0 / math.sqrt(128)
 
     def seq_at(dy, dx):
@@ -65,6 +68,12 @@
     for dy, dx in shifts:
         pl.semaphore_signal(
             barrier, inc=1, device_id={"seq": seq_at(dy, dx)}, device_id_type=pl.DeviceIdType.MESH
+        )
+        pl.semaphore_signal(
+            barrier,
+            inc=1,
+            device_id={"seq": seq_at(dy, dx), "kvh": other},
+            device_id_type=pl.DeviceIdType.MESH,
         )
     for e in range(1, 8):
         pl.semaphore_signal(
@@ -218,7 +227,7 @@
             send_v[(h // 2) * 4 + t, h % 2] = a[t * 16 : t * 16 + 16]
 
     with jax.named_scope("barrier"):
-        pl.semaphore_wait(barrier, 22)
+        pl.semaphore_wait(barrier, 37)
 
     def remote(src, dst, send_sem, recv_sem, where):
         return pltpu.make_async_remote_copy(
@@ -227,51 +236,85 @@
         )
 
     order = sorted(shifts, key=lambda d: -(min(d[0], 4 - d[0]) + min(d[1], 4 - d[1])))
-    for dy, dx in order:
+
+    def give(dy, dx):
         d = dy * 4 + dx
         peer = seq_at(dy, dx)
-        for push in (
-            remote(zsend_v.at[peer // 4], zrecv_v.at[d], rz_s, rz_r, {"seq": peer}),
-            remote(send_v.at[peer], recv_v.at[d], rs_s, rs_r, {"seq": peer}),
-        ):
-            push.start()
-    recv_v[0] = send_v[seq]
-    zrecv_v[0] = zsend_v[sy]
-    with jax.named_scope("rs_recv"):
-        wait_for(zrecv_v.at[pl.ds(1, 15)], rz_r)
-        wait_for(recv_v.at[pl.ds(1, 15)], rs_r)
-    pick = where_true(iota((16, 128), 1) == iota((16, 128), 0) + 16 * sx)
-    heads = []
-    for e in range(2):
-        z = jnp.concatenate([zrecv_v[d, e : e + 1, :] for d in range(16)], axis=0)
-        f = jnp.exp(z - jnp.max(z, axis=0, keepdims=True))
-        f = jnp.where(iota((16, 128), 1) < 64, f, 0.0)
-        whole = jnp.sum(f * pltpu.roll(z, 64, 1), axis=0, keepdims=True)
-        g = jnp.where(iota((16, 128), 1) < 64, f / whole, 0.0)
-        g_hi = g.astype(BF16)
-        g_lo = (g - g_hi.astype(F32)).astype(BF16)
-        share = dot_nt(pick, g_hi) + dot_nt(pick, g_lo)
-        found = jnp.zeros((16, 128), F32)
-        for d in range(16):
-            part = jnp.where(iota((16, 16), 1) == d, share, 0.0)
-            found = found + recv_v[d, e].astype(F32) * jnp.sum(part, axis=1, keepdims=True)
-        piece_v[e] = found.astype(BF16)
+        at = {"seq": peer, "kvh": keeper}
+        remote(
+            zsend_v.at[peer // 4], zrecv_v.at[core, d], rz_s, rz_r.at[core], at
+        ).start()
+        remote(send_v.at[peer], recv_v.at[core, d], rs_s, rs_r.at[core], at).start()
+
+    for dy, dx in order:
+        give(dy, dx)
+
+    @pl.when(core == 0)
+    def _():
+        give(0, 0)
 
     def place(o):
         return att_v.at[pl.ds(2 * (o // 4), 2), pl.ds(pl.multiple_of(16 * (o % 4), 16), 16), :]
 
-    for dy, dx in order:
-        remote(piece_v, place(seq), ag_s, ag_r.at[dy], {"seq": seq_at(dy, dx)}).start()
-    place(seq)[...] = piece_v[...]
-    wait_for(zrecv_v.at[pl.ds(1, 15)], rz_s)
-    wait_for(send_v.at[pl.ds(1, 15)], rs_s)
+    def combined(group):
+        heads = []
+        for e in range(2):
+            z = jnp.concatenate([zrecv_v[group, d, e : e + 1, :] for d in range(16)], axis=0)
+            f = jnp.exp(z - jnp.max(z, axis=0, keepdims=True))
+            f = jnp.where(iota((16, 128), 1) < 64, f, 0.0)
+            whole = jnp.sum(f * pltpu.roll(z, 64, 1), axis=0, keepdims=True)
+            g = jnp.where(iota((16, 128), 1) < 64, f / whole, 0.0)
+            g_hi = g.astype(BF16)
+            g_lo = (g - g_hi.astype(F32)).astype(BF16)
+            share = dot_nt(pick, g_hi) + dot_nt(pick, g_lo)
+            found = jnp.zeros((16, 128), F32)
+            for d in range(16):
+                part = jnp.where(iota((16, 16), 1) == d, share, 0.0)
+                found = found + recv_v[group, d, e].astype(F32) * jnp.sum(
+                    part, axis=1, keepdims=True
+                )
+            piece_v[group, e] = found.astype(BF16)
+
+    pick = where_true(iota((16, 128), 1) == iota((16, 128), 0) + 16 * sx)
+
+    @pl.when(core == 1)
+    def _():
+        with jax.named_scope("rs_recv0"):
+            wait_for(zrecv_v.at[0], rz_r.at[0])
+            wait_for(recv_v.at[0], rs_r.at[0])
+        combined(0)
+        for dy, dx in order + [(0, 0)]:
+            at = {"seq": seq_at(dy, dx), "kvh": other}
+            remote(piece_v.at[0], place(seq), ag_s.at[0], ag_r.at[dy], at).start()
+        recv_v[1, 0] = send_v[seq]
+        zrecv_v[1, 0] = zsend_v[sy]
+        with jax.named_scope("rs_recv1"):
+            wait_for(zrecv_v.at[1, pl.ds(1, 15)], rz_r.at[1])
+            wait_for(recv_v.at[1, pl.ds(1, 15)], rs_r.at[1])
+        combined(1)
+        for dy, dx in order:
+            at = {"seq": seq_at(dy, dx)}
+            remote(piece_v.at[1], place(seq), ag_s.at[1], ag_r.at[dy], at).start()
+        place(seq)[...] = piece_v[1]
+
     l_w.wait()
 
     terms = None
     for dy in (0, 1, 3, 2):
         y = lax.rem(sy - dy + 4, 4)
         with jax.named_scope(f"ag_recv{dy}"):
-            wait_for(att_v.at[pl.ds(2 * y, 2), pl.ds(0, 64 if dy else 48)], ag_r.at[dy])
+            if dy:
+                wait_for(att_v.at[pl.ds(2 * y, 2)], ag_r.at[dy])
+            else:
+
+                @pl.when(core == 0)
+                def _():
+                    wait_for(att_v.at[pl.ds(2 * y, 2)], ag_r.at[0])
+
+                @pl.when(core == 1)
+                def _():
+                    wait_for(att_v.at[pl.ds(2 * y, 2), pl.ds(0, 48)], ag_r.at[0])
+
         for e in range(2):
             term = dot(att_v[2 * y + e], w_v[2 * y + e])
             terms = term if terms is None else terms + term
@@ -280,7 +323,19 @@
     for e in (4, 5, 3, 6, 2, 7, 1):
         peer = lax.rem(kvh + e, 8)
         remote(psend_v.at[peer], precv_v.at[e], pj_s, pj_r, {"kvh": peer}).start()
-    wait_for(recv_v.at[pl.ds(1, 15)], ag_s)
+
+    @pl.when(core == 0)
+    def _():
+        wait_for(zrecv_v.at[0], rz_s)
+        wait_for(recv_v.at[0], rs_s)
+
+    @pl.when(core == 1)
+    def _():
+        wait_for(zrecv_v.at[1, pl.ds(1, 15)], rz_s)
+        wait_for(recv_v.at[1, pl.ds(1, 15)], rs_s)
+        wait_for(recv_v.at[0], ag_s.at[0])
+        wait_for(recv_v.at[1, pl.ds(1, 15)], ag_s.at[1])
+
     result = psend_v[kvh].astype(F32)
     with jax.named_scope("pj_recv"):
         wait_for(precv_v.at[pl.ds(1, 7)], pj_r)
@@ -309,10 +364,10 @@
             vmem((9 * STRIDE, 128), F32), vmem((512, 128), F32), vmem((8, 256), F32),
             vmem((3, 64, 256), BF16), vmem((128, 128), F32), vmem((16, 128), F32),
             vmem((8, 128), F32),
-            vmem((16, 2, 16, 128), BF16), vmem((16, 2, 16, 128), BF16),
-            vmem((4, 2, 128), F32), vmem((16, 2, 128), F32), vmem((2, 16, 128), BF16),
+            vmem((16, 2, 16, 128), BF16), vmem((2, 16, 2, 16, 128), BF16),
+            vmem((4, 2, 128), F32), vmem((2, 16, 2, 128), F32), vmem((2, 2, 16, 128), BF16),
             vmem((8, 64, 128), BF16), vmem((8, 8, 512), BF16), vmem((8, 8, 512), BF16),
-            dma((6,)), dma, dma, dma, dma, dma, dma, dma((4,)), dma, dma,
+            dma((6,)), dma, dma, dma((2,)), dma, dma((2,)), dma((2,)), dma((4,)), dma, dma,
         ],
         compiler_params=pltpu.CompilerParams(collective_id=0, has_side_effects=True, vmem_limit_bytes=24 * 1024 * 1024),
         name="decode",

time: 25.7 us -> 25 us (0.973)
  Pallas kernels: 25 us -> 24.3 us
    pallas_call x1, Pallas kernels: 25 us -> 24.3 us  [on_device(): pl.pallas_call(kernel, out_shape=jax.ShapeDtypeStruct((8, 512), BF16), in...]
where the time goes in v5:
time: 25 us; the launch traced here: 24.9 us
  Pallas kernels  24.3 us (97%)
  local copies, waits for them, and re-layouts  0.6 us (2%)
    pallas_call x1, Pallas kernels, on_device(): pl.pallas_call(kernel, out_shape=jax.ShapeDtypeStruct((8, 512), BF16), in...  24.3 us
    unnamed x1, local copies, waits for them, and re-layouts  0.6 us

profile of v5, /device:TPU:1, one launch (start us, length us, event | category | flops | bytes accessed | tf_op | source)
XLA Modules:
  0.0 24.9 jit_solution(6660894863927357014)
XLA Ops:
  0.0 24.3 %decode.1 = bf16[8,512]{1,0:T(8,128)(2,1)S(1)} custom-call(bf16[512,128]{1,0:T(8,128)(2,1)} %bitcast.12, bf16[128,128,128]{2,1,0:T(8,128)(2,1)} %bitcast.9, bf16[128,128,128]{2,1,0:T(8,128)(2,1)} %bitcast.10, bf16[512,128]{1,0:T(8,128)(2,1)} %bitcast.13, bf16[512,128]{1,0:T(8,128)(2,1)} %bitcast.14, s32[16,64]{1,0:T(8,128)} %bitcast.15, s32[128]{0:T(128)} %cnt_hbm.1, ...), custom_call_target="tpu_custom_call" | custom-call | tf_op jit(solution)/shard_map/decode/pallas_call | solution.py:352
  24.3 0.6 %copy.10 = bf16[8,512]{1,0:T(8,128)(2,1)} copy(bf16[8,512]{1,0:T(8,128)(2,1)S(1)} %decode.1) | data formatting | bytes 16384

commit v6 on v5

--- a/solution.py
+++ b/solution.py
@@ -285,7 +285,7 @@
         combined(0)
         for dy, dx in order + [(0, 0)]:
             at = {"seq": seq_at(dy, dx), "kvh": other}
-            remote(piece_v.at[0], place(seq), ag_s.at[0], ag_r.at[dy], at).start()
+            remote(piece_v.at[0], place(seq), ag_s.at[0], ag_r.at[sx], at).start()
         recv_v[1, 0] = send_v[seq]
         zrecv_v[1, 0] = zsend_v[sy]
         with jax.named_scope("rs_recv1"):
@@ -294,35 +294,34 @@
         combined(1)
         for dy, dx in order:
             at = {"seq": seq_at(dy, dx)}
-            remote(piece_v.at[1], place(seq), ag_s.at[1], ag_r.at[dy], at).start()
+            remote(piece_v.at[1], place(seq), ag_s.at[1], ag_r.at[sx], at).start()
         place(seq)[...] = piece_v[1]
 
     l_w.wait()
 
-    terms = None
-    for dy in (0, 1, 3, 2):
-        y = lax.rem(sy - dy + 4, 4)
-        with jax.named_scope(f"ag_recv{dy}"):
-            if dy:
-                wait_for(att_v.at[pl.ds(2 * y, 2)], ag_r.at[dy])
-            else:
-
-                @pl.when(core == 0)
-                def _():
-                    wait_for(att_v.at[pl.ds(2 * y, 2)], ag_r.at[0])
-
-                @pl.when(core == 1)
-                def _():
-                    wait_for(att_v.at[pl.ds(2 * y, 2), pl.ds(0, 48)], ag_r.at[0])
-
-        for e in range(2):
-            term = dot(att_v[2 * y + e], w_v[2 * y + e])
-            terms = term if terms is None else terms + term
-    for e in range(8):
-        psend_v[e] = terms[e * 8 : e * 8 + 8, :].astype(BF16)
-    for e in (4, 5, 3, 6, 2, 7, 1):
-        peer = lax.rem(kvh + e, 8)
-        remote(psend_v.at[peer], precv_v.at[e], pj_s, pj_r, {"kvh": peer}).start()
+    for c in range(4):
+        tokens = pl.ds(16 * c, 16)
+        short = (core == 1) & (sx == c)
+        with jax.named_scope(f"ag_recv{c}"):
+
+            @pl.when(short)
+            def _():
+                wait_for(att_v.at[pl.ds(0, 6), tokens], ag_r.at[c])
+
+            @pl.when(jnp.logical_not(short))
+            def _():
+                wait_for(att_v.at[:, tokens], ag_r.at[c])
+
+        rows = jnp.concatenate([att_v[h, 16 * c : 16 * c + 16, :] for h in range(8)], axis=1)
+        terms = dot(rows, w_v[...])
+        for i in range(2):
+            peer = 2 * c + i
+            psend_v[peer] = terms[i * 8 : i * 8 + 8].astype(BF16)
+            e = lax.rem(peer - kvh + 8, 8)
+
+            @pl.when(kvh != peer)
+            def _():
+                remote(psend_v.at[peer], precv_v.at[e], pj_s, pj_r, {"kvh": peer}).start()
 
     @pl.when(core == 0)
     def _():
@@ -357,7 +356,7 @@
         scratch_shapes=[
             vmem((3, 512, 128), BF16), vmem((128, 128, 128), BF16), vmem((128, 128, 128), BF16),
             vmem((16, 64), jnp.int32),
-            vmem((8, 128, 512), BF16), smem((128,), jnp.int32), vmem((16, 128), jnp.int32),
+            vmem((1024, 512), BF16), smem((128,), jnp.int32), vmem((16, 128), jnp.int32),
             smem((16, 128), jnp.int32),
             vmem((16, 128), F32), vmem((64, 8, 128), F32), vmem((520, 128), F32),
             vmem((512, 128), BF16), vmem((512, 512), F32), vmem((512, 512), BF16), vmem((CAP // 4, 32, 256), BF16),
@@ -379,7 +378,7 @@
         rep_values.reshape(-1, rep_values.shape[3]),
         jnp.transpose(block_ids, (1, 2, 0)).reshape(block_ids.shape[2], block_ids.shape[0]),
         block_counts,
-        out_weight.reshape(8, 128, out_weight.shape[1]),
+        out_weight,
     )])
 
 

time: 25 us -> 24.5 us (0.980)
  Pallas kernels: 24.3 us -> 23.8 us
    pallas_call x1, Pallas kernels: 24.3 us -> 23.8 us  [on_device(): pl.pallas_call(kernel, out_shape=jax.ShapeDtypeStruct((8, 512), BF16), in...]
where the time goes in v6:
time: 24.5 us; the launch traced here: 24.4 us
  Pallas kernels  23.8 us (97%)
  local copies, waits for them, and re-layouts  0.6 us (2%)
    pallas_call x1, Pallas kernels, on_device(): pl.pallas_call(kernel, out_shape=jax.ShapeDtypeStruct((8, 512), BF16), in...  23.8 us
    unnamed x1, local copies, waits for them, and re-layouts  0.6 us

profile of v6, /device:TPU:1, one launch (start us, length us, event | category | flops | bytes accessed | tf_op | source)
XLA Modules:
  0.0 24.4 jit_solution(2197224549555857451)
XLA Ops:
  0.0 23.8 %decode.1 = bf16[8,512]{1,0:T(8,128)(2,1)S(1)} custom-call(bf16[512,128]{1,0:T(8,128)(2,1)} %bitcast.10, bf16[128,128,128]{2,1,0:T(8,128)(2,1)} %bitcast.8, bf16[128,128,128]{2,1,0:T(8,128)(2,1)} %bitcast.9, bf16[512,128]{1,0:T(8,128)(2,1)} %bitcast.11, bf16[512,128]{1,0:T(8,128)(2,1)} %bitcast.12, s32[16,64]{1,0:T(8,128)} %bitcast.13, s32[128]{0:T(128)} %cnt_hbm.1, ...), custom_call_target="tpu_custom_call" | custom-call | tf_op jit(solution)/shard_map/decode/pallas_call | solution.py:351
  23.8 0.6 %copy.10 = bf16[8,512]{1,0:T(8,128)(2,1)} copy(bf16[8,512]{1,0:T(8,128)(2,1)S(1)} %decode.1) | data formatting | bytes 16384

commit v7 on v6

--- a/solution.py
+++ b/solution.py
@@ -246,12 +246,12 @@
         ).start()
         remote(send_v.at[peer], recv_v.at[core, d], rs_s, rs_r.at[core], at).start()
 
-    for dy, dx in order:
-        give(dy, dx)
-
-    @pl.when(core == 0)
-    def _():
-        give(0, 0)
+    for c in range(4):
+        for dy in (2, 1, 3, 0):
+
+            @pl.when((core == 0) | (sx != c) | (dy != 0))
+            def _():
+                give(dy, lax.rem(c - sx + 4, 4))
 
     def place(o):
         return att_v.at[pl.ds(2 * (o // 4), 2), pl.ds(pl.multiple_of(16 * (o % 4), 16), 16), :]
@@ -259,7 +259,7 @@
     def combined(group):
         heads = []
         for e in range(2):
-            z = jnp.concatenate([zrecv_v[group, d, e : e + 1, :] for d in range(16)], axis=0)
+            z = zrecv_v[group, :, e, :]
             f = jnp.exp(z - jnp.max(z, axis=0, keepdims=True))
             f = jnp.where(iota((16, 128), 1) < 64, f, 0.0)
             whole = jnp.sum(f * pltpu.roll(z, 64, 1), axis=0, keepdims=True)
@@ -279,13 +279,6 @@
 
     @pl.when(core == 1)
     def _():
-        with jax.named_scope("rs_recv0"):
-            wait_for(zrecv_v.at[0], rz_r.at[0])
-            wait_for(recv_v.at[0], rs_r.at[0])
-        combined(0)
-        for dy, dx in order + [(0, 0)]:
-            at = {"seq": seq_at(dy, dx), "kvh": other}
-            remote(piece_v.at[0], place(seq), ag_s.at[0], ag_r.at[sx], at).start()
         recv_v[1, 0] = send_v[seq]
         zrecv_v[1, 0] = zsend_v[sy]
         with jax.named_scope("rs_recv1"):
@@ -296,6 +289,13 @@
             at = {"seq": seq_at(dy, dx)}
             remote(piece_v.at[1], place(seq), ag_s.at[1], ag_r.at[sx], at).start()
         place(seq)[...] = piece_v[1]
+        with jax.named_scope("rs_recv0"):
+            wait_for(zrecv_v.at[0], rz_r.at[0])
+            wait_for(recv_v.at[0], rs_r.at[0])
+        combined(0)
+        for dy, dx in order + [(0, 0)]:
+            at = {"seq": seq_at(dy, dx), "kvh": other}
+            remote(piece_v.at[0], place(seq), ag_s.at[0], ag_r.at[sx], at).start()
 
     l_w.wait()
 

time: 24.5 us -> 24.3 us (level)
  no operation moved by 1% of the time
where the time goes in v7:
time: 24.3 us; the launch traced here: 24.2 us
  Pallas kernels  23.6 us (97%)
  local copies, waits for them, and re-layouts  0.6 us (2%)
    pallas_call x1, Pallas kernels, on_device(): pl.pallas_call(kernel, out_shape=jax.ShapeDtypeStruct((8, 512), BF16), in...  23.6 us
    unnamed x1, local copies, waits for them, and re-layouts  0.6 us

profile of v7, /device:TPU:1, one launch (start us, length us, event | category | flops | bytes accessed | tf_op | source)
XLA Modules:
  0.0 24.2 jit_solution(8001947611704419055)
XLA Ops:
  0.0 23.6 %decode.1 = bf16[8,512]{1,0:T(8,128)(2,1)S(1)} custom-call(bf16[512,128]{1,0:T(8,128)(2,1)} %bitcast.10, bf16[128,128,128]{2,1,0:T(8,128)(2,1)} %bitcast.8, bf16[128,128,128]{2,1,0:T(8,128)(2,1)} %bitcast.9, bf16[512,128]{1,0:T(8,128)(2,1)} %bitcast.11, bf16[512,128]{1,0:T(8,128)(2,1)} %bitcast.12, s32[16,64]{1,0:T(8,128)} %bitcast.13, s32[128]{0:T(128)} %cnt_hbm.1, ...), custom_call_target="tpu_custom_call" | custom-call | tf_op jit(solution)/shard_map/decode/pallas_call | solution.py:351
  23.6 0.6 %copy.10 = bf16[8,512]{1,0:T(8,128)(2,1)} copy(bf16[8,512]{1,0:T(8,128)(2,1)S(1)} %decode.1) | data formatting | bytes 16384

commit v8 on v7

--- a/solution.py
+++ b/solution.py
@@ -211,6 +211,30 @@
     for y in range(4):
         zsend_v[y, :, 0:64] = high[2 * y : 2 * y + 2]
         zsend_v[y, :, 64:128] = sums[2 * y : 2 * y + 2]
+    with jax.named_scope("barrier"):
+        pl.semaphore_wait(barrier, 37)
+
+    def remote(src, dst, send_sem, recv_sem, where):
+        return pltpu.make_async_remote_copy(
+            src_ref=src, dst_ref=dst, send_sem=send_sem, recv_sem=recv_sem,
+            device_id=where, device_id_type=pl.DeviceIdType.MESH,
+        )
+
+    order = sorted(shifts, key=lambda d: -(min(d[0], 4 - d[0]) + min(d[1], 4 - d[1])))
+
+    def tell(dy, dx):
+        peer = seq_at(dy, dx)
+        at = {"seq": peer, "kvh": keeper}
+        source = zsend_v.at[peer // 4]
+        remote(source, zrecv_v.at[core, dy * 4 + dx], rz_s, rz_r.at[core], at).start()
+
+    for dy, dx in shifts:
+        tell(dy, dx)
+
+    @pl.when(core == 0)
+    def _():
+        tell(0, 0)
+
     col_m = col_v[0:64, 0:8]
     high_col = jnp.where(
         tmap_v[2][:, 0:8].astype(F32) > 0.0, dot_nt(first_b, most), col_m.astype(BF16).astype(F32)
@@ -226,24 +250,10 @@
         for t in range(4):
             send_v[(h // 2) * 4 + t, h % 2] = a[t * 16 : t * 16 + 16]
 
-    with jax.named_scope("barrier"):
-        pl.semaphore_wait(barrier, 37)
-
-    def remote(src, dst, send_sem, recv_sem, where):
-        return pltpu.make_async_remote_copy(
-            src_ref=src, dst_ref=dst, send_sem=send_sem, recv_sem=recv_sem,
-            device_id=where, device_id_type=pl.DeviceIdType.MESH,
-        )
-
-    order = sorted(shifts, key=lambda d: -(min(d[0], 4 - d[0]) + min(d[1], 4 - d[1])))
-
     def give(dy, dx):
         d = dy * 4 + dx
         peer = seq_at(dy, dx)
         at = {"seq": peer, "kvh": keeper}
-        remote(
-            zsend_v.at[peer // 4], zrecv_v.at[core, d], rz_s, rz_r.at[core], at
-        ).start()
         remote(send_v.at[peer], recv_v.at[core, d], rs_s, rs_r.at[core], at).start()
 
     for c in range(4):

time: 24.3 us -> 24.3 us (level)
  no operation moved by 1% of the time
where the time goes in v8:
time: 24.3 us; the launch traced here: 24.2 us
  Pallas kernels  23.6 us (97%)
  local copies, waits for them, and re-layouts  0.6 us (2%)
    pallas_call x1, Pallas kernels, on_device(): pl.pallas_call(kernel, out_shape=jax.ShapeDtypeStruct((8, 512), BF16), in...  23.6 us
    unnamed x1, local copies, waits for them, and re-layouts  0.6 us

profile of v8, /device:TPU:1, one launch (start us, length us, event | category | flops | bytes accessed | tf_op | source)
XLA Modules:
  0.0 24.2 jit_solution(4056896947988785859)
XLA Ops:
  0.0 23.6 %decode.1 = bf16[8,512]{1,0:T(8,128)(2,1)S(1)} custom-call(bf16[512,128]{1,0:T(8,128)(2,1)} %bitcast.10, bf16[128,128,128]{2,1,0:T(8,128)(2,1)} %bitcast.8, bf16[128,128,128]{2,1,0:T(8,128)(2,1)} %bitcast.9, bf16[512,128]{1,0:T(8,128)(2,1)} %bitcast.11, bf16[512,128]{1,0:T(8,128)(2,1)} %bitcast.12, s32[16,64]{1,0:T(8,128)} %bitcast.13, s32[128]{0:T(128)} %cnt_hbm.1, ...), custom_call_target="tpu_custom_call" | custom-call | tf_op jit(solution)/shard_map/decode/pallas_call | solution.py:361
  23.6 0.6 %copy.10 = bf16[8,512]{1,0:T(8,128)(2,1)} copy(bf16[8,512]{1,0:T(8,128)(2,1)S(1)} %decode.1) | data formatting | bytes 16384

commit v9 on v8

--- a/solution.py
+++ b/solution.py
@@ -34,7 +34,7 @@
     small_v, k_v, v_v, ids_v, w_v, cnt_s, slot_v, slot_s,
     wide_v, q3, q32, qh_v, rs_v, rp_v, weight_v, acc_v, summed_v, seg_v,
     tmap_v, col_v, row_v, cnt_v, send_v, recv_v, zsend_v, zrecv_v, piece_v, att_v, psend_v, precv_v,
-    in_sem, slot_sem, rs_s, rs_r, rz_s, rz_r, ag_s, ag_r, pj_s, pj_r,
+    in_sem, slot_sem, rs_s, rs_r, rz_s, rz_r, ag_s, ag_r, pj_s, pj_r, w_s, w_r,
 ):
     seq = lax.axis_index("seq")
     kvh = lax.axis_index("kvh")
@@ -55,7 +55,7 @@
         for src, dst, i in [
             (ids_hbm, ids_v, 0), (cnt_hbm, cnt_s, 1), (q_hbm, small_v.at[0], 2),
             (rk_hbm, small_v.at[1], 2), (rv_hbm, small_v.at[2], 2), (k_hbm, k_v, 3),
-            (v_hbm, v_v, 4), (w_hbm, w_v, 5),
+            (v_hbm, v_v, 4), (w_hbm, w_v.at[1], 5),
         ]
     ]
     for load in loads:
@@ -263,9 +263,6 @@
             def _():
                 give(dy, lax.rem(c - sx + 4, 4))
 
-    def place(o):
-        return att_v.at[pl.ds(2 * (o // 4), 2), pl.ds(pl.multiple_of(16 * (o % 4), 16), 16), :]
-
     def combined(group):
         heads = []
         for e in range(2):
@@ -287,72 +284,87 @@
 
     pick = where_true(iota((16, 128), 1) == iota((16, 128), 0) + 16 * sx)
 
+    hand = remote(w_v.at[1], w_v.at[0], w_s, w_r, {"kvh": keeper})
+    l_w.wait()
+
+    @pl.when(core == 0)
+    def _():
+        hand.start()
+
     @pl.when(core == 1)
     def _():
+        def place(group, o):
+            return att_v.at[
+                group, pl.ds(2 * (o // 4), 2), pl.ds(pl.multiple_of(16 * (o % 4), 16), 16), :
+            ]
+
+        def spread(group):
+            combined(group)
+            for dy, dx in order:
+                at = {"seq": seq_at(dy, dx)}
+                remote(
+                    piece_v.at[group], place(group, seq), ag_s, ag_r.at[sx], at
+                ).start()
+            place(group, seq)[...] = piece_v[group]
+
         recv_v[1, 0] = send_v[seq]
         zrecv_v[1, 0] = zsend_v[sy]
         with jax.named_scope("rs_recv1"):
             wait_for(zrecv_v.at[1, pl.ds(1, 15)], rz_r.at[1])
             wait_for(recv_v.at[1, pl.ds(1, 15)], rs_r.at[1])
-        combined(1)
-        for dy, dx in order:
-            at = {"seq": seq_at(dy, dx)}
-            remote(piece_v.at[1], place(seq), ag_s.at[1], ag_r.at[sx], at).start()
-        place(seq)[...] = piece_v[1]
+        spread(1)
         with jax.named_scope("rs_recv0"):
             wait_for(zrecv_v.at[0], rz_r.at[0])
             wait_for(recv_v.at[0], rs_r.at[0])
-        combined(0)
-        for dy, dx in order + [(0, 0)]:
-            at = {"seq": seq_at(dy, dx), "kvh": other}
-            remote(piece_v.at[0], place(seq), ag_s.at[0], ag_r.at[sx], at).start()
-
-    l_w.wait()
-
-    for c in range(4):
-        tokens = pl.ds(16 * c, 16)
-        short = (core == 1) & (sx == c)
-        with jax.named_scope(f"ag_recv{c}"):
-
-            @pl.when(short)
-            def _():
-                wait_for(att_v.at[pl.ds(0, 6), tokens], ag_r.at[c])
-
-            @pl.when(jnp.logical_not(short))
-            def _():
-                wait_for(att_v.at[:, tokens], ag_r.at[c])
-
-        rows = jnp.concatenate([att_v[h, 16 * c : 16 * c + 16, :] for h in range(8)], axis=1)
-        terms = dot(rows, w_v[...])
-        for i in range(2):
-            peer = 2 * c + i
-            psend_v[peer] = terms[i * 8 : i * 8 + 8].astype(BF16)
-            e = lax.rem(peer - kvh + 8, 8)
-
-            @pl.when(kvh != peer)
-            def _():
-                remote(psend_v.at[peer], precv_v.at[e], pj_s, pj_r, {"kvh": peer}).start()
+        spread(0)
+        hand.wait_recv()
+
+        for c in range(4):
+            tokens = pl.ds(16 * c, 16)
+            with jax.named_scope(f"ag_recv{c}"):
+
+                @pl.when(sx == c)
+                def _():
+                    wait_for(att_v.at[:, pl.ds(0, 6), tokens], ag_r.at[c])
+
+                @pl.when(sx != c)
+                def _():
+                    wait_for(att_v.at[:, :, tokens], ag_r.at[c])
+
+            terms = None
+            for g in range(2):
+                rows = [att_v[g, h, 16 * c : 16 * c + 16, :] for h in range(8)]
+                term = dot(jnp.concatenate(rows, axis=1), w_v[g])
+                terms = term if terms is None else terms + term
+            for i in range(2):
+                peer = 2 * c + i
+                psend_v[peer] = terms[i * 8 : i * 8 + 8].astype(BF16)
+
+                @pl.when(kvh != peer)
+                def _():
+                    remote(
+                        psend_v.at[peer], precv_v.at[kvh // 2], pj_s, pj_r, {"kvh": peer}
+                    ).start()
+
+        precv_v[kvh // 2] = psend_v[kvh]
+        wait_for(zrecv_v.at[1, pl.ds(1, 15)], rz_s)
+        wait_for(recv_v.at[1, pl.ds(1, 15)], rs_s)
+        wait_for(recv_v.at[:, pl.ds(1, 15)], ag_s)
+        wait_for(precv_v.at[pl.ds(0, 3)], pj_r)
+        wait_for(psend_v.at[pl.ds(1, 7)], pj_s)
 
     @pl.when(core == 0)
     def _():
         wait_for(zrecv_v.at[0], rz_s)
         wait_for(recv_v.at[0], rs_s)
-
-    @pl.when(core == 1)
-    def _():
-        wait_for(zrecv_v.at[1, pl.ds(1, 15)], rz_s)
-        wait_for(recv_v.at[1, pl.ds(1, 15)], rs_s)
-        wait_for(recv_v.at[0], ag_s.at[0])
-        wait_for(recv_v.at[1, pl.ds(1, 15)], ag_s.at[1])
-
-    result = psend_v[kvh].astype(F32)
-    with jax.named_scope("pj_recv"):
-        wait_for(precv_v.at[pl.ds(1, 7)], pj_r)
-    for e in range(1, 8):
-        result = result + precv_v[e].astype(F32)
+        hand.wait_send()
+        with jax.named_scope("pj_recv"):
+            wait_for(precv_v, pj_r)
+
+    result = precv_v[0].astype(F32)
+    for z in range(1, 4):
+        result = result + precv_v[z].astype(F32)
     out_ref[...] = result.astype(BF16)
-    with jax.named_scope("pj_send"):
-        wait_for(psend_v.at[pl.ds(1, 7)], pj_s)
 
 
 def on_device(queries, keys, values, rep_keys, rep_values, block_ids, block_counts, out_weight):
@@ -366,7 +378,7 @@
         scratch_shapes=[
             vmem((3, 512, 128), BF16), vmem((128, 128, 128), BF16), vmem((128, 128, 128), BF16),
             vmem((16, 64), jnp.int32),
-            vmem((1024, 512), BF16), smem((128,), jnp.int32), vmem((16, 128), jnp.int32),
+            vmem((2, 1024, 512), BF16), smem((128,), jnp.int32), vmem((16, 128), jnp.int32),
             smem((16, 128), jnp.int32),
             vmem((16, 128), F32), vmem((64, 8, 128), F32), vmem((520, 128), F32),
             vmem((512, 128), BF16), vmem((512, 512), F32), vmem((512, 512), BF16), vmem((CAP // 4, 32, 256), BF16),
@@ -375,8 +387,8 @@
             vmem((8, 128), F32),
             vmem((16, 2, 16, 128), BF16), vmem((2, 16, 2, 16, 128), BF16),
             vmem((4, 2, 128), F32), vmem((2, 16, 2, 128), F32), vmem((2, 2, 16, 128), BF16),
-            vmem((8, 64, 128), BF16), vmem((8, 8, 512), BF16), vmem((8, 8, 512), BF16),
-            dma((6,)), dma, dma, dma((2,)), dma, dma((2,)), dma((2,)), dma((4,)), dma, dma,
+            vmem((2, 8, 64, 128), BF16), vmem((8, 8, 512), BF16), vmem((4, 8, 512), BF16),
+            dma((6,)), dma, dma, dma((2,)), dma, dma((2,)), dma, dma((4,)), dma, dma, dma, dma,
         ],
         compiler_params=pltpu.CompilerParams(collective_id=0, has_side_effects=True, vmem_limit_bytes=24 * 1024 * 1024),
         name="decode",

time: 24.3 us -> 23.6 us (0.971)
  Pallas kernels: 23.6 us -> 22.9 us
    pallas_call x1, Pallas kernels: 23.6 us -> 22.9 us  [on_device(): pl.pallas_call(kernel, out_shape=jax.ShapeDtypeStruct((8, 512), BF16), in...]
where the time goes in v9:
time: 23.6 us; the launch traced here: 23.5 us
  Pallas kernels  22.9 us (97%)
  local copies, waits for them, and re-layouts  0.6 us (3%)
    pallas_call x1, Pallas kernels, on_device(): pl.pallas_call(kernel, out_shape=jax.ShapeDtypeStruct((8, 512), BF16), in...  22.9 us
    unnamed x1, local copies, waits for them, and re-layouts  0.6 us

profile of v9, /device:TPU:1, one launch (start us, length us, event | category | flops | bytes accessed | tf_op | source)
XLA Modules:
  0.0 23.5 jit_solution(3083777959111917258)
XLA Ops:
  0.0 22.9 %decode.1 = bf16[8,512]{1,0:T(8,128)(2,1)S(1)} custom-call(bf16[512,128]{1,0:T(8,128)(2,1)} %bitcast.10, bf16[128,128,128]{2,1,0:T(8,128)(2,1)} %bitcast.8, bf16[128,128,128]{2,1,0:T(8,128)(2,1)} %bitcast.9, bf16[512,128]{1,0:T(8,128)(2,1)} %bitcast.11, bf16[512,128]{1,0:T(8,128)(2,1)} %bitcast.12, s32[16,64]{1,0:T(8,128)} %bitcast.13, s32[128]{0:T(128)} %cnt_hbm.1, ...), custom_call_target="tpu_custom_call" | custom-call | tf_op jit(solution)/shard_map/decode/pallas_call | solution.py:373
  22.9 0.6 %copy.10 = bf16[8,512]{1,0:T(8,128)(2,1)} copy(bf16[8,512]{1,0:T(8,128)(2,1)S(1)} %decode.1) | data formatting | bytes 16384

commit v10 on v9

--- a/solution.py
+++ b/solution.py
@@ -303,7 +303,7 @@
             for dy, dx in order:
                 at = {"seq": seq_at(dy, dx)}
                 remote(
-                    piece_v.at[group], place(group, seq), ag_s, ag_r.at[sx], at
+                    piece_v.at[group], place(group, seq), ag_s, ag_r.at[group, sx], at
                 ).start()
             place(group, seq)[...] = piece_v[group]
 
@@ -321,18 +321,17 @@
 
         for c in range(4):
             tokens = pl.ds(16 * c, 16)
-            with jax.named_scope(f"ag_recv{c}"):
+            terms = None
+            for g in (1, 0):
 
                 @pl.when(sx == c)
                 def _():
-                    wait_for(att_v.at[:, pl.ds(0, 6), tokens], ag_r.at[c])
+                    wait_for(att_v.at[g, pl.ds(0, 6), tokens], ag_r.at[g, c])
 
                 @pl.when(sx != c)
                 def _():
-                    wait_for(att_v.at[:, :, tokens], ag_r.at[c])
-
-            terms = None
-            for g in range(2):
+                    wait_for(att_v.at[g, :, tokens], ag_r.at[g, c])
+
                 rows = [att_v[g, h, 16 * c : 16 * c + 16, :] for h in range(8)]
                 term = dot(jnp.concatenate(rows, axis=1), w_v[g])
                 terms = term if terms is None else terms + term
@@ -388,7 +387,7 @@
             vmem((16, 2, 16, 128), BF16), vmem((2, 16, 2, 16, 128), BF16),
             vmem((4, 2, 128), F32), vmem((2, 16, 2, 128), F32), vmem((2, 2, 16, 128), BF16),
             vmem((2, 8, 64, 128), BF16), vmem((8, 8, 512), BF16), vmem((4, 8, 512), BF16),
-            dma((6,)), dma, dma, dma((2,)), dma, dma((2,)), dma, dma((4,)), dma, dma, dma, dma,
+            dma((6,)), dma, dma, dma((2,)), dma, dma((2,)), dma, dma((2, 4)), dma, dma, dma, dma,
         ],
         compiler_params=pltpu.CompilerParams(collective_id=0, has_side_effects=True, vmem_limit_bytes=24 * 1024 * 1024),
         name="decode",

time: 23.6 us -> 23.6 us (level)
  no operation moved by 1% of the time
where the time goes in v10:
time: 23.6 us; the launch traced here: 23.5 us
  Pallas kernels  22.9 us (97%)
  local copies, waits for them, and re-layouts  0.6 us (3%)
    pallas_call x1, Pallas kernels, on_device(): pl.pallas_call(kernel, out_shape=jax.ShapeDtypeStruct((8, 512), BF16), in...  22.9 us
    unnamed x1, local copies, waits for them, and re-layouts  0.6 us

profile of v10, /device:TPU:1, one launch (start us, length us, event | category | flops | bytes accessed | tf_op | source)
XLA Modules:
  0.0 23.5 jit_solution(8062614844197584998)
XLA Ops:
  0.0 22.9 %decode.1 = bf16[8,512]{1,0:T(8,128)(2,1)S(1)} custom-call(bf16[512,128]{1,0:T(8,128)(2,1)} %bitcast.10, bf16[128,128,128]{2,1,0:T(8,128)(2,1)} %bitcast.8, bf16[128,128,128]{2,1,0:T(8,128)(2,1)} %bitcast.9, bf16[512,128]{1,0:T(8,128)(2,1)} %bitcast.11, bf16[512,128]{1,0:T(8,128)(2,1)} %bitcast.12, s32[16,64]{1,0:T(8,128)} %bitcast.13, s32[128]{0:T(128)} %cnt_hbm.1, ...), custom_call_target="tpu_custom_call" | custom-call | tf_op jit(solution)/shard_map/decode/pallas_call | solution.py:372
  22.9 0.6 %copy.10 = bf16[8,512]{1,0:T(8,128)(2,1)} copy(bf16[8,512]{1,0:T(8,128)(2,1)S(1)} %decode.1) | data formatting | bytes 16384
